TPU v7x, 64 devices: a 2x2x8 block of a 4x4x8 slice. The times are simulated.
64 devices in a mesh: rep: 8 (over x, y, core), dp: 8 (over z).
Axes of the slice: x: 2, y: 2, z: 8, core: 2. Of those that a mesh axis runs over, the one named last changes fastest.
The devices are a block of a 4x4x8 slice.
Arguments:
- x: bfloat16 [64, 4096, 512], P(('rep', 'dp')), parts along dimension 0
- dy: bfloat16 [64, 4096, 512], P(('rep', 'dp')), parts along dimension 0
- w_gate: bfloat16 [2, 512, 2048], replicated
- w_up: bfloat16 [2, 512, 2048], replicated
- w_down: bfloat16 [2, 2048, 512], replicated
- m_w_gate: float32 [2, 512, 2048], P(None, 'dp')
- m_w_up: float32 [2, 512, 2048], P(None, 'dp')
- m_w_down: float32 [2, 2048, 512], P(None, 'dp')
- v_w_gate: float32 [2, 512, 2048], P(None, 'dp')
- v_w_up: float32 [2, 512, 2048], P(None, 'dp')
- v_w_down: float32 [2, 2048, 512], P(None, 'dp')
Outputs:
- output 1: bfloat16 [16, 512, 2048], P('rep'), parts along dimension 0
- output 2: bfloat16 [16, 512, 2048], P('rep'), parts along dimension 0
- output 3: bfloat16 [16, 2048, 512], P('rep'), parts along dimension 0
- output 4: float32 [16, 512, 2048], P('rep', 'dp'), parts along dimension 0
- output 5: float32 [16, 512, 2048], P('rep', 'dp'), parts along dimension 0
- output 6: float32 [16, 2048, 512], P('rep', 'dp'), parts along dimension 0
- output 7: float32 [16, 512, 2048], P('rep', 'dp'), parts along dimension 0
- output 8: float32 [16, 512, 2048], P('rep', 'dp'), parts along dimension 0
- output 9: float32 [16, 2048, 512], P('rep', 'dp'), parts along dimension 0
There are 8 independent parts. A program takes and returns all parts, laid end to end along the dimension named above; an argument that names none is the same for every part.
All inputs are finite; a program needn't handle non-finite values.
Results may differ from a plain program's by a relative error of at most 0.022.
Values are sent between devices in bfloat16 or wider.
A program may use at most 768 MiB of HBM per device.

v0:
```python
import jax
import jax.numpy as jnp
from jax import lax

NAMES = ("w_gate", "w_up", "w_down")


def matmul(a, w):
    return jnp.dot(a, w, preferred_element_type=jnp.float32).astype(jnp.bfloat16)


def normed(h):
    wide = h.astype(jnp.float32)
    scale = lax.rsqrt(jnp.mean(wide**2, -1, keepdims=True) + 1e-6)
    return (wide * scale).astype(jnp.bfloat16)


def layer(h, w):
    a = normed(h)
    gate = jnp.dot(a, w["w_gate"], preferred_element_type=jnp.float32)
    up = jnp.dot(a, w["w_up"], preferred_element_type=jnp.float32)
    return h + matmul((jax.nn.silu(gate) * up).astype(jnp.bfloat16), w["w_down"])


def adamw(w, m, v, g):
    m = 0.9 * m + 0.1 * g
    v = 0.95 * v + 0.05 * g * g
    step = m * lax.rsqrt(v + 1e-8) + 0.1 * w
    return (w - 0.02 * step).astype(jnp.bfloat16), m, v


def clipped(gradients, sum_of_squares, count):
    factor = jnp.minimum(1.0, 0.5 * lax.rsqrt(sum_of_squares / count + 1e-30))
    return [g * factor for g in gradients]


def stack(weights, h):
    for number in range(weights["w_gate"].shape[0]):
        h = layer(h, {name: w[number] for name, w in weights.items()})
    return h


def solution(mesh):
    groups = mesh.shape["rep"]

    def step(x, dy, *arrays):
        weights, m, v = (arrays[i : i + 3] for i in (0, 3, 6))
        x, dy = (t.reshape(groups, -1, *t.shape[1:]) for t in (x, dy))

        def of_a_group(x, dy):
            _, back = jax.vjp(lambda w: stack(w, x), dict(zip(NAMES, weights, strict=True)))
            by_weights = back(dy)[0]
            gradients = [by_weights[name].astype(jnp.float32) for name in NAMES]
            gradients = clipped(gradients, sum(jnp.sum(g * g) for g in gradients), sum(g.size for g in gradients))
            new = [adamw(w.astype(jnp.float32), m, v, g) for w, m, v, g in zip(weights, m, v, gradients, strict=True)]
            return tuple(one[which] for which in range(3) for one in new)

        return tuple(t.reshape(-1, *t.shape[2:]) for t in jax.vmap(of_a_group)(x, dy))

    return step
```

profile of v0, /device:TPU:22, one launch (start us, length us, event | category | flops | bytes accessed | tf_op | source)
XLA Modules:
  0.0 941.7 jit_solution(17865249632329950302)
XLA Ops:
  23.2 15.1 %convolution_convert_fusion.1 = bf16[4096,2048]{1,0:T(8,128)(2,1)} fusion(bf16[1,4096,512]{2,1,0:T(8,128)(2,1)} %param.17, bf16[2,2048,512]{2,1,0:T(8,128)(2,1)} %param.16), kind=kOutput, calls=%fused_computation.201 | convolution fusion | flops 8598323200 | bytes 23068672 | tf_op jit(solution)/vmap(transpose(jvp()))/dot_general | solution.py:9
  38.3 16.5 %fusion.215 = f32[4096,2048]{1,0:T(8,128)} fusion(bf16[2,512,2048]{2,1,0:T(8,128)(2,1)} %param.12, bf16[1,4096,512]{2,1,0:T(8,128)(2,1)S(1)} %copy-done.13, f32[4096]{0:T(1024)S(1)} %add_rsqrt_fusion), kind=kOutput, calls=%fused_computation.241 | convolution fusion | flops 8596226048 | bytes 39862272 | tf_op jit(solution)/vmap(jvp())/dot_general | solution.py:20
  54.8 31.4 %fusion.164 = (bf16[1,1,4096,2048]{3,2,1,0:T(8,128)(2,1)}, f32[4096,2048]{1,0:T(8,128)}) fusion(f32[4096,2048]{1,0:T(8,128)} %fusion.215, bf16[2,512,2048]{2,1,0:T(8,128)(2,1)} %param.15, bf16[1,4096,512]{2,1,0:T(8,128)(2,1)S(1)} %copy-done.13, f32[4096]{0:T(1024)S(1)} %add_rsqrt_fusion), kind=kOutput, calls=%fused_computation.191 | convolution fusion | flops 8646557696 | bytes 90193920 | tf_op jit(solution)/vmap(jvp())/dot_general | solution.py:21
  86.2 21.1 %copy.4 = bf16[1,1,4096,2048]{2,3,1,0:T(8,128)(2,1)} copy(bf16[1,1,4096,2048]{3,2,1,0:T(8,128)(2,1)} %get-tuple-element.263) | data formatting | bytes 33554432
  107.3 16.0 %fusion.174 = (f32[4096]{0:T(1024)S(1)}, bf16[1,1,4096,512]{2,3,1,0:T(8,128)(2,1)}) fusion(bf16[2,2048,512]{2,1,0:T(8,128)(2,1)} %param.16, bf16[1,1,4096,2048]{3,2,1,0:T(8,128)(2,1)} %get-tuple-element.263, bf16[1,4096,512]{1,2,0:T(8,128)(2,1)} %copy), kind=kOutput, calls=%fused_computation.213 | convolution fusion | flops 8600416256 | bytes 27279360 | tf_op jit(solution)/vmap(jvp())/dot_general | solution.py:9
  129.4 15.5 %fusion.203 = f32[4096,2048]{1,0:T(8,128)} fusion(bf16[1,1,4096,512]{2,3,1,0:T(8,128)(2,1)S(1)} %fusion.175, bf16[2,512,2048]{2,1,0:T(8,128)(2,1)S(1)} %copy-done.28), kind=kOutput, calls=%fused_computation.229 | convolution fusion | flops 8589934592 | bytes 39845888 | tf_op jit(solution)/vmap(jvp())/dot_general | solution.py:21
  144.9 44.8 %fusion.153 = (bf16[1,1,4096,2048]{3,2,1,0:T(8,128)(2,1)}, bf16[1,1,4096,2048]{3,2,1,0:T(8,128)(2,1)}, f32[4096,2048]{1,0:T(8,128)}) fusion(f32[4096,2048]{1,0:T(8,128)} %fusion.203, bf16[4096,2048]{1,0:T(8,128)(2,1)} %convolution_convert_fusion.1, bf16[2,512,2048]{2,1,0:T(8,128)(2,1)} %param.12, bf16[1,1,4096,512]{2,3,1,0:T(8,128)(2,1)} %copy-done.2), kind=kOutput, calls=%fused_computation.175 | convolution fusion | flops 8715763712 | bytes 123731968 | tf_op jit(solution)/vmap(jvp())/dot_general | solution.py:20
  189.7 14.6 %fusion.180 = bf16[4096,512]{0,1:T(8,128)(2,1)} fusion(bf16[1,1,4096,2048]{3,2,1,0:T(8,128)(2,1)} %get-tuple-element.622, bf16[2,512,2048]{2,1,0:T(8,128)(2,1)} %param.15), kind=kOutput, calls=%fused_computation.218 | convolution fusion | flops 8589934592 | bytes 23068672 | tf_op jit(solution)/vmap(transpose(jvp()))/dot_general | solution.py:21
  204.3 14.5 %fusion.176 = (f32[4096]{0:T(1024)S(1)}, bf16[1,1,4096,512]{2,3,1,0:T(8,128)(2,1)S(1)}) fusion(bf16[1,1,4096,512]{2,3,1,0:T(8,128)(2,1)S(1)} %copy-done.14, bf16[4096,512]{0,1:T(8,128)(2,1)} %fusion.180, bf16[2,512,2048]{2,1,0:T(8,128)(2,1)} %param.12, bf16[1,1,4096,2048]{3,2,1,0:T(8,128)(2,1)} %get-tuple-element.544), kind=kOutput, calls=%fused_computation.215 | convolution fusion | flops 8600416256 | bytes 31473664 | tf_op jit(solution)/vmap(transpose(jvp()))/dot_general | solution.py:20
  229.6 63.8 %while.17 = (bf16[1,1,4096,2048]{2,3,1,0:T(8,128)(2,1)}, bf16[1,1,4096,512]{3,2,1,0:T(8,128)(2,1)}, f32[1,256,512]{2,1,0:T(8,128)S(1)}, f32[1,256,512]{2,1,0:T(8...) while((bf16[1,1,4096,2048]{2,3,1,0:T(8,128)(2,1)}, ...), condition=%wide.windowed_dot_general_cond_rs.5.clone, body=%wide.windowed_dot_general_body_rs.5.clone.sunk | while | flops 4312530944 | bytes 144704176 | solution.py:9
  254.9 8.8 collective-permute-done.22
  294.3 27.7 %fusion.163 = bf16[1,1,4096,2048]{3,2,1,0:T(8,128)(2,1)} fusion(f32[4096,2048]{1,0:T(8,128)} %fusion.203, f32[4096,2048]{1,0:T(8,128)} %get-tuple-element.267), kind=kLoop, calls=%fused_computation.189 | loop fusion | flops 50331648 | bytes 83886080 | tf_op jit(solution)/vmap(jvp())/convert_element_type | solution.py:22
  322.0 21.3 %copy.2 = bf16[1,1,4096,2048]{2,3,1,0:T(8,128)(2,1)} copy(bf16[1,1,4096,2048]{3,2,1,0:T(8,128)(2,1)} %fusion.163) | data formatting | bytes 33554432
  349.8 52.1 %while.16 = (bf16[1,1,4096,2048]{2,3,1,0:T(8,128)(2,1)}, bf16[1,1,4096,512]{3,2,1,0:T(8,128)(2,1)}, f32[1,256,512]{2,1,0:T(8,128)S(1)}, f32[1,256,512]{2,1,0:T(8...) while((bf16[1,1,4096,2048]{2,3,1,0:T(8,128)(2,1)}, ...), condition=%wide.windowed_dot_general_cond_rs.4.clone, body=%wide.windowed_dot_general_body_rs.4.clone.sunk | while | flops 4312530944 | bytes 144704176 | solution.py:9
  408.5 40.9 %convert_multiply_fusion = (bf16[1,1,4096,2048]{3,2,1,0:T(8,128)(2,1)}, bf16[1,1,4096,2048]{3,2,1,0:T(8,128)(2,1)}) fusion(f32[4096,2048]{1,0:T(8,128)} %fusion.215, f32[4096,2048]{1,0:T(8,128)} %get-tuple-element.264, bf16[2,2048,512]{2,1,0:T(8,128)(2,1)} %param.16, bf16[1,1,4096,512]{2,3,1,0:T(8,128)(2,1)} %fusion.198), kind=kOutput, calls=%fused_computation.170 | convolution fusion | flops 8724152320 | bytes 106954752 | tf_op jit(solution)/vmap(transpose(jvp()))/dot_general | solution.py:9
  449.4 66.4 %while.15 = (bf16[1,1,4096,512]{2,3,1,0:T(8,128)(2,1)}, bf16[1,1,4096,2048]{3,2,1,0:T(8,128)(2,1)}, f32[1,64,2048]{2,1,0:T(8,128)S(1)}, f32[1,64,2048]{2,1,0:T(8...) while((bf16[1,1,4096,512]{2,3,1,0:T(8,128)(2,1)}, ...), condition=%wide.windowed_dot_general_cond_rs.3.clone, body=%wide.windowed_dot_general_body_rs.3.clone.sunk | while | flops 4299948032 | bytes 60818020 | solution.py:21
  517.5 75.1 %while.14 = (bf16[1,1,4096,512]{2,3,1,0:T(8,128)(2,1)}, bf16[1,1,4096,2048]{3,2,1,0:T(8,128)(2,1)}, f32[1,64,2048]{2,1,0:T(8,128)S(1)}, f32[1,64,2048]{2,1,0:T(8...) while((bf16[1,1,4096,512]{2,3,1,0:T(8,128)(2,1)}, ...), condition=%wide.windowed_dot_general_cond_rs.2.clone, body=%wide.windowed_dot_general_body_rs.2.clone.sunk | while | flops 4299948032 | bytes 62915200 | solution.py:21
  593.4 60.1 %while.13 = (bf16[1,1,4096,512]{2,3,1,0:T(8,128)(2,1)}, bf16[1,1,4096,2048]{3,2,1,0:T(8,128)(2,1)}, f32[1,64,2048]{2,1,0:T(8,128)S(1)}, f32[1,64,2048]{2,1,0:T(8...) while((bf16[1,1,4096,512]{2,3,1,0:T(8,128)(2,1)}, ...), condition=%wide.windowed_dot_general_cond_rs.1.clone, body=%wide.windowed_dot_general_body_rs.1.clone.sunk | while | flops 4299948032 | bytes 62915200 | solution.py:20
  629.4 8.4 fusion.327
  654.3 70.8 %while.12 = (bf16[1,1,4096,512]{2,3,1,0:T(8,128)(2,1)}, bf16[1,1,4096,2048]{3,2,1,0:T(8,128)(2,1)}, f32[1,64,2048]{2,1,0:T(8,128)S(1)}, f32[1,64,2048]{2,1,0:T(8...) while((bf16[1,1,4096,512]{2,3,1,0:T(8,128)(2,1)}, ...), condition=%wide.windowed_dot_general_cond_rs.clone, body=%wide.windowed_dot_general_body_rs.clone.sunk | while | flops 4299948032 | bytes 62915200 | solution.py:20
  749.9 15.3 %all-reduce.10 = f32[1]{0:T(128)} all-reduce(f32[1]{0:T(128)} %bitcast.39), channel_id=13, replica_groups=mesh['rep'=8,'dp'=8] {'dp'}, use_global_device_ids=true, to_apply=%region_3.4.clone | all-reduce | flops 1 | bytes 8 | tf_op jit(solution)/vmap()/reduce_sum | solution.py:54
  777.2 44.3 %all-gather.14.cloned.1.call-done = bf16[1,2,2048,512]{3,2,1,0:T(8,128)(2,1)} async-done(((bf16[1,2,256,512]{3,2,1,0:T(8,128)(2,1)}), bf16[1,2,2048,512]{3,2,1,0:T(8,128)(2,1)}) %all-gather.14.cloned.1.call-update) | async-done | bytes 4194320 | tf_op jit(solution)/reshape | solution.py:58
  821.5 52.1 %all-gather.12.cloned.1.call-done = bf16[1,2,512,2048]{3,2,1,0:T(8,128)(2,1)} async-done(((bf16[1,2,64,2048]{3,2,1,0:T(8,128)(2,1)}), bf16[1,2,512,2048]{3,2,1,0:T(8,128)(2,1)}) %all-gather.12.cloned.1.call-update) | async-done | bytes 4194320 | tf_op jit(solution)/reshape | solution.py:58
  873.6 52.2 %all-gather.10.cloned.1.call-done = bf16[1,2,512,2048]{3,2,1,0:T(8,128)(2,1)} async-done(((bf16[1,2,64,2048]{3,2,1,0:T(8,128)(2,1)}), bf16[1,2,512,2048]{3,2,1,0:T(8,128)(2,1)}) %all-gather.10.cloned.1.call-update) | async-done | bytes 4194320 | tf_op jit(solution)/reshape | solution.py:58
  (310 shorter events, 439.6 us)
Async XLA Ops:
  7.2 814.3 %all-gather.14.cloned.1.call-start = ((), (), s32[]{:S(2)}) async-start(), calls=%async_computation.2 | async-start | bytes 4718592 | tf_op jit(solution)/reshape | solution.py:58
  229.7 19.4 %collective-permute-start.20 = (f32[1,256,512]{2,1,0:T(8,128)S(1)}, f32[1,256,512]{2,1,0:T(8,128)S(1)}, u32[]{:S(2)}, u32[]{:S(2)}) collective-permute-start(f32[1,256,512]{2,1,0:T(8,128)S(1)} %broadcast_select_fusion.34), channel_id=35, source_target_pairs={{0,1},{1,2},{2,3},{3,4},{4,5},{5,6},{6,7},{7,0},{8,9},{9,10},{10,1... | collective-permute-start | bytes 1572872 | tf_op jit(solution)/vmap(transpose(jvp()))/dot_general | solution.py:9
  231.9 17.1 %collective-permute-start.21 = (f32[1,256,512]{2,1,0:T(8,128)S(1)}, f32[1,256,512]{2,1,0:T(8,128)S(1)}, u32[]{:S(2)}, u32[]{:S(2)}) collective-permute-start(f32[1,256,512]{2,1,0:T(8,128)S(1)} %broadcast_select_fusion.35), channel_id=34, source_target_pairs={{0,7},{1,0},{2,1},{3,2},{4,3},{5,4},{6,5},{7,6},{8,15},{9,8},{10,9... | collective-permute-start | bytes 1572872 | tf_op jit(solution)/vmap(transpose(jvp()))/dot_general | solution.py:9
  249.3 14.5 %collective-permute-start.22 = (f32[1,256,512]{2,1,0:T(8,128)S(1)}, f32[1,256,512]{2,1,0:T(8,128)S(1)}, u32[]{:S(2)}, u32[]{:S(2)}) collective-permute-start(f32[1,256,512]{2,1,0:T(8,128)S(1)} %get-tuple-element.500), channel_id=37, source_target_pairs={{0,1},{1,2},{2,3},{3,4},{4,5},{5,6},{6,7},{7,0},{8,9},{9,10},{10,1... | collective-permute-start | bytes 1572872 | tf_op jit(solution)/vmap(transpose(jvp()))/dot_general | solution.py:9
  293.4 433.1 %collective-permute-start.29 = (f32[1,256,512]{2,1,0:T(8,128)}, f32[1,256,512]{2,1,0:T(8,128)}, u32[]{:S(2)}, u32[]{:S(2)}) collective-permute-start(f32[1,256,512]{2,1,0:T(8,128)} %get-tuple-element.47), channel_id=38, source_target_pairs={{0,1},{1,2},{2,3},{3,4},{4,5},{5,6},{6,7},{7,0},{8,9},{9,10},{10,1... | collective-permute-start | bytes 1572872 | tf_op jit(solution)/vmap(transpose(jvp()))/dot_general | solution.py:9
  401.9 327.4 %collective-permute-start.28 = (f32[1,256,512]{2,1,0:T(8,128)}, f32[1,256,512]{2,1,0:T(8,128)}, u32[]{:S(2)}, u32[]{:S(2)}) collective-permute-start(f32[1,256,512]{2,1,0:T(8,128)} %get-tuple-element.45), channel_id=32, source_target_pairs={{0,1},{1,2},{2,3},{3,4},{4,5},{5,6},{6,7},{7,0},{8,9},{9,10},{10,1... | collective-permute-start | bytes 1572872 | tf_op jit(solution)/vmap(transpose(jvp()))/dot_general | solution.py:9
  449.5 14.5 %collective-permute-start.12 = (f32[1,64,2048]{2,1,0:T(8,128)S(1)}, f32[1,64,2048]{2,1,0:T(8,128)S(1)}, u32[]{:S(2)}, u32[]{:S(2)}) collective-permute-start(f32[1,64,2048]{2,1,0:T(8,128)S(1)} %broadcast_select_fusion.30), channel_id=22, source_target_pairs={{0,1},{1,2},{2,3},{3,4},{4,5},{5,6},{6,7},{7,0},{8,9},{9,10},{10,1... | collective-permute-start | bytes 1572872 | tf_op jit(solution)/vmap(transpose(jvp()))/dot_general | solution.py:21
  481.1 15.2 %collective-permute-start.12 = (f32[1,64,2048]{2,1,0:T(8,128)S(1)}, f32[1,64,2048]{2,1,0:T(8,128)S(1)}, u32[]{:S(2)}, u32[]{:S(2)}) collective-permute-start(f32[1,64,2048]{2,1,0:T(8,128)S(1)} %broadcast_select_fusion.30), channel_id=22, source_target_pairs={{0,1},{1,2},{2,3},{3,4},{4,5},{5,6},{6,7},{7,0},{8,9},{9,10},{10,1... | collective-permute-start | bytes 1572872 | tf_op jit(solution)/vmap(transpose(jvp()))/dot_general | solution.py:21
  481.2 16.0 %collective-permute-start.13 = (f32[1,64,2048]{2,1,0:T(8,128)S(1)}, f32[1,64,2048]{2,1,0:T(8,128)S(1)}, u32[]{:S(2)}, u32[]{:S(2)}) collective-permute-start(f32[1,64,2048]{2,1,0:T(8,128)S(1)} %broadcast_select_fusion.31), channel_id=21, source_target_pairs={{0,7},{1,0},{2,1},{3,2},{4,3},{5,4},{6,5},{7,6},{8,15},{9,8},{10,9... | collective-permute-start | bytes 1572872 | tf_op jit(solution)/vmap(transpose(jvp()))/dot_general | solution.py:21
  498.2 16.0 %collective-permute-start.14 = (f32[1,64,2048]{2,1,0:T(8,128)}, f32[1,64,2048]{2,1,0:T(8,128)S(1)}, u32[]{:S(2)}, u32[]{:S(2)}) collective-permute-start(f32[1,64,2048]{2,1,0:T(8,128)} %get-tuple-element.482), channel_id=24, source_target_pairs={{0,1},{1,2},{2,3},{3,4},{4,5},{5,6},{6,7},{7,0},{8,9},{9,10},{10,1... | collective-permute-start | bytes 1572872 | tf_op jit(solution)/vmap(transpose(jvp()))/dot_general | solution.py:21
  515.8 214.6 %collective-permute-start.27 = (f32[1,64,2048]{2,1,0:T(8,128)}, f32[1,64,2048]{2,1,0:T(8,128)}, u32[]{:S(2)}, u32[]{:S(2)}) collective-permute-start(f32[1,64,2048]{2,1,0:T(8,128)} %get-tuple-element.43), channel_id=25, source_target_pairs={{0,1},{1,2},{2,3},{3,4},{4,5},{5,6},{6,7},{7,0},{8,9},{9,10},{10,1... | collective-permute-start | bytes 1572872 | tf_op jit(solution)/vmap(transpose(jvp()))/dot_general | solution.py:21
  518.6 18.8 %collective-permute-start.8 = (f32[1,64,2048]{2,1,0:T(8,128)}, f32[1,64,2048]{2,1,0:T(8,128)}, u32[]{:S(2)}, u32[]{:S(2)}) collective-permute-start(f32[1,64,2048]{2,1,0:T(8,128)} %broadcast_select_fusion.28), channel_id=16, source_target_pairs={{0,1},{1,2},{2,3},{3,4},{4,5},{5,6},{6,7},{7,0},{8,9},{9,10},{10,1... | collective-permute-start | bytes 1572872 | tf_op jit(solution)/vmap(transpose(jvp()))/dot_general | solution.py:21
  521.5 15.9 %collective-permute-start.9 = (f32[1,64,2048]{2,1,0:T(8,128)}, f32[1,64,2048]{2,1,0:T(8,128)S(1)}, u32[]{:S(2)}, u32[]{:S(2)}) collective-permute-start(f32[1,64,2048]{2,1,0:T(8,128)} %broadcast_select_fusion.29), channel_id=15, source_target_pairs={{0,7},{1,0},{2,1},{3,2},{4,3},{5,4},{6,5},{7,6},{8,15},{9,8},{10,9... | collective-permute-start | bytes 1572872 | tf_op jit(solution)/vmap(transpose(jvp()))/dot_general | solution.py:21
  539.5 15.4 %collective-permute-start.10 = (f32[1,64,2048]{2,1,0:T(8,128)}, f32[1,64,2048]{2,1,0:T(8,128)S(1)}, u32[]{:S(2)}, u32[]{:S(2)}) collective-permute-start(f32[1,64,2048]{2,1,0:T(8,128)} %get-tuple-element.473), channel_id=18, source_target_pairs={{0,1},{1,2},{2,3},{3,4},{4,5},{5,6},{6,7},{7,0},{8,9},{9,10},{10,1... | collective-permute-start | bytes 1572872 | tf_op jit(solution)/vmap(transpose(jvp()))/dot_general | solution.py:21
  540.1 15.6 %collective-permute-start.11 = (f32[1,64,2048]{2,1,0:T(8,128)}, f32[1,64,2048]{2,1,0:T(8,128)}, u32[]{:S(2)}, u32[]{:S(2)}) collective-permute-start(f32[1,64,2048]{2,1,0:T(8,128)} %get-tuple-element.474), channel_id=17, source_target_pairs={{0,7},{1,0},{2,1},{3,2},{4,3},{5,4},{6,5},{7,6},{8,15},{9,8},{10,9... | collective-permute-start | bytes 1572872 | tf_op jit(solution)/vmap(transpose(jvp()))/dot_general | solution.py:21
  559.7 15.1 %collective-permute-start.8 = (f32[1,64,2048]{2,1,0:T(8,128)}, f32[1,64,2048]{2,1,0:T(8,128)}, u32[]{:S(2)}, u32[]{:S(2)}) collective-permute-start(f32[1,64,2048]{2,1,0:T(8,128)} %broadcast_select_fusion.28), channel_id=16, source_target_pairs={{0,1},{1,2},{2,3},{3,4},{4,5},{5,6},{6,7},{7,0},{8,9},{9,10},{10,1... | collective-permute-start | bytes 1572872 | tf_op jit(solution)/vmap(transpose(jvp()))/dot_general | solution.py:21
  655.4 15.1 %collective-permute-start = (f32[1,64,2048]{2,1,0:T(8,128)}, f32[1,64,2048]{2,1,0:T(8,128)}, u32[]{:S(2)}, u32[]{:S(2)}) collective-permute-start(f32[1,64,2048]{2,1,0:T(8,128)} %broadcast_select_fusion.24), channel_id=3, source_target_pairs={{0,1},{1,2},{2,3},{3,4},{4,5},{5,6},{6,7},{7,0},{8,9},{9,10},{10,1... | collective-permute-start | bytes 1572872 | tf_op jit(solution)/vmap(transpose(jvp()))/dot_general | solution.py:20
  689.1 15.1 %collective-permute-start = (f32[1,64,2048]{2,1,0:T(8,128)}, f32[1,64,2048]{2,1,0:T(8,128)}, u32[]{:S(2)}, u32[]{:S(2)}) collective-permute-start(f32[1,64,2048]{2,1,0:T(8,128)} %broadcast_select_fusion.24), channel_id=3, source_target_pairs={{0,1},{1,2},{2,3},{3,4},{4,5},{5,6},{6,7},{7,0},{8,9},{9,10},{10,1... | collective-permute-start | bytes 1572872 | tf_op jit(solution)/vmap(transpose(jvp()))/dot_general | solution.py:20
  706.3 16.0 %collective-permute-start.2 = (f32[1,64,2048]{2,1,0:T(8,128)}, f32[1,64,2048]{2,1,0:T(8,128)S(1)}, u32[]{:S(2)}, u32[]{:S(2)}) collective-permute-start(f32[1,64,2048]{2,1,0:T(8,128)} %get-tuple-element.455), channel_id=5, source_target_pairs={{0,1},{1,2},{2,3},{3,4},{4,5},{5,6},{6,7},{7,0},{8,9},{9,10},{10,1... | collective-permute-start | bytes 1572872 | tf_op jit(solution)/vmap(transpose(jvp()))/dot_general | solution.py:20
  706.3 16.8 %collective-permute-start.3 = (f32[1,64,2048]{2,1,0:T(8,128)}, f32[1,64,2048]{2,1,0:T(8,128)}, u32[]{:S(2)}, u32[]{:S(2)}) collective-permute-start(f32[1,64,2048]{2,1,0:T(8,128)} %get-tuple-element.456), channel_id=4, source_target_pairs={{0,7},{1,0},{2,1},{3,2},{4,3},{5,4},{6,5},{7,6},{8,15},{9,8},{10,9... | collective-permute-start | bytes 1572872 | tf_op jit(solution)/vmap(transpose(jvp()))/dot_general | solution.py:20
  726.4 14.9 %collective-permute-start.25 = (f32[1,64,2048]{2,1,0:T(8,128)}, f32[1,64,2048]{2,1,0:T(8,128)S(1)}, u32[]{:S(2)}, u32[]{:S(2)}) collective-permute-start(f32[1,64,2048]{2,1,0:T(8,128)} %copy-done.15), channel_id=12, source_target_pairs={{0,1},{1,2},{2,3},{3,4},{4,5},{5,6},{6,7},{7,0},{8,9},{9,10},{10,1... | collective-permute-start | bytes 1572872 | tf_op jit(solution)/vmap(transpose(jvp()))/dot_general | solution.py:20
  726.5 20.4 %collective-permute-start.24 = (f32[1,64,2048]{2,1,0:T(8,128)}, f32[1,64,2048]{2,1,0:T(8,128)S(1)}, u32[]{:S(2)}, u32[]{:S(2)}) collective-permute-start(f32[1,64,2048]{2,1,0:T(8,128)} %get-tuple-element.37), channel_id=6, source_target_pairs={{0,1},{1,2},{2,3},{3,4},{4,5},{5,6},{6,7},{7,0},{8,9},{9,10},{10,1... | collective-permute-start | bytes 1572872 | tf_op jit(solution)/vmap(transpose(jvp()))/dot_general | solution.py:20
  769.7 103.9 %all-gather.12.cloned.1.call-start = ((), (), s32[]{:S(2)}) async-start(), calls=%async_computation.1 | async-start | bytes 4718592 | tf_op jit(solution)/reshape | solution.py:58
  773.3 152.5 %all-gather.10.cloned.1.call-start = ((), (), s32[]{:S(2)}) async-start(), calls=%async_computation | async-start | bytes 4718592 | tf_op jit(solution)/reshape | solution.py:58
  (70 other events, 973.5 us)
Sparse Core Ops, SparseCore 0:
  769.9 51.5 all-gather.13
  823.6 49.9 all-gather.11
  875.8 49.9 all-gather.9
where the time goes:
time: 954 us; the launch traced here: 942 us
  matrix products  377 us (40%)
  waiting for transfers between devices  217 us (23%)
  other arithmetic  107 us (11%)
  local copies, waits for them, and re-layouts  94 us (10%)
  starting transfers between devices  90.2 us (9%)
  loops' own time  23.8 us (2%)
  between operations  17.5 us (2%)
  blocking collectives  15.3 us (2%)
    reshape x3, waiting for transfers between devices, step(): t.reshape(-1, *t.shape[2:])  149 us
    dot_general x11, matrix products, layer(): gate = jnp.dot(a, w['w_gate'], preferred_element_type=jnp.float32)  143 us
    dot_general x11, matrix products, layer(): up = jnp.dot(a, w['w_up'], preferred_element_type=jnp.float32)  129 us
    dot_general x11, matrix products, matmul(): jnp.dot(a, w, preferred_element_type=jnp.float32).astype(jnp.bfloat16)  105 us
    unnamed x55, local copies, waits for them, and re-layouts  81.6 us
    dot_general x18, starting transfers between devices, matmul(): jnp.dot(a, w, preferred_element_type=jnp.float32).astype(jnp.bfloat16)  33.9 us
    dot_general x18, waiting for transfers between devices, matmul(): jnp.dot(a, w, preferred_element_type=jnp.float32).astype(jnp.bfloat16)  33.6 us
    dot_general x18, starting transfers between devices, layer(): up = jnp.dot(a, w['w_up'], preferred_element_type=jnp.float32)  28.2 us
  transfers between devices with their start and end apart: 57, of which 25 were waited for; matrix products, arithmetic and copies ran while one was open for 35% of the time, Pallas kernels for 0%

commit v1 on v0

v1 whole, which is shorter than its diff:
```python
import functools

import jax
import jax.numpy as jnp
from jax import lax
from jax.experimental import pallas as pl
from jax.experimental.pallas import tpu as pltpu
from jax.sharding import PartitionSpec as P

F32, BF16 = jnp.float32, jnp.bfloat16
TT = 512
LB = 128
VMEM_LIMIT = 67_043_328


def dot(a, b):
    return jnp.dot(a, b, preferred_element_type=F32)


def rms(wide):
    return lax.rsqrt(jnp.mean(wide * wide, -1, keepdims=True) + 1e-6)


def sigmoid(g):
    return 0.5 * jnp.tanh(0.5 * g) + 0.5


def grad_kernel(cfg, x_h, dy_h, wg_h, wu_h, wd_h, gg_h, gu_h, gd_h, a1_h, a1t_h,
                w1, w1d, w2, w2d, wgut, wdt, a, at, h1, dy, dyt, da, xb, hid, pg, pd, ob, od,
                sem_w, sem_x, sem_dy, sem_a, sem_at, sem_o):
    nt, nc, n = cfg
    half = nc // 2
    fc = 2 * LB

    def blocks(j):
        c = 2 * (j % half) + j // half
        return c, c + nc

    for layer, (wgu, wdn) in enumerate(((w1, w1d), (w2, w2d))):
        for j in range(nc):
            for s, b in enumerate(blocks(j)):
                cols, rows = pl.ds(b * LB, LB), pl.ds(s * LB, LB)
                pltpu.make_async_copy(wg_h.at[layer, :, cols], wgu.at[j, :, rows], sem_w.at[layer, 0]).start()
                pltpu.make_async_copy(wu_h.at[layer, :, cols], wgu.at[j, :, pl.ds(fc + s * LB, LB)], sem_w.at[layer, 0]).start()
                pltpu.make_async_copy(wd_h.at[layer, cols, :], wdn.at[j * 2 + s], sem_w.at[layer, 1]).start()

    def x_copy(t):
        return pltpu.make_async_copy(x_h.at[0, pl.ds(t * TT, TT), :], xb.at[t % 2], sem_x.at[t % 2])

    def dy_copy(t):
        return pltpu.make_async_copy(dy_h.at[0, pl.ds(t * TT, TT), :], dy.at[t], sem_dy.at[t])

    x_copy(0).start()
    for t in range(nt):
        dy_copy(t).start()
    pltpu.make_async_copy(w1, w1, sem_w.at[0, 0]).wait()
    pltpu.make_async_copy(w1d, w1d, sem_w.at[0, 1]).wait()

    @pl.loop(0, nt)
    def _(t):
        x_copy(t).wait()

        @pl.when(t + 1 < nt)
        def _():
            x_copy(t + 1).start()

        wide = xb[t % 2].astype(F32)
        a1 = (wide * rms(wide)).astype(BF16)
        a[t] = a1
        at[t] = a1.T
        pltpu.make_async_copy(a.at[t], a1_h.at[t], sem_a.at[t]).start()
        pltpu.make_async_copy(at.at[t], a1t_h.at[t], sem_at.at[t]).start()
        for j in range(nc):
            gu = dot(a1, w1[j])
            g, u = gu[:, :fc], gu[:, fc:]
            hid[:, j * fc:(j + 1) * fc] = (g * sigmoid(g) * u).astype(BF16)
        y = dot(hid[...], w1d[...].reshape(2 * nc * LB, -1))
        h1[t] = (xb[t % 2].astype(F32) + y.astype(BF16).astype(F32)).astype(BF16)
        da[t] = jnp.zeros(da.shape[1:], F32)
        dy_copy(t).wait()
        dyt[t] = dy[t].T

    pltpu.make_async_copy(w2, w2, sem_w.at[1, 0]).wait()
    pltpu.make_async_copy(w2d, w2d, sem_w.at[1, 1]).wait()

    @pl.loop(0, nt)
    def _(t):
        pltpu.make_async_copy(a.at[t], a1_h.at[t], sem_a.at[t]).wait()
        pltpu.make_async_copy(at.at[t], a1t_h.at[t], sem_at.at[t]).wait()
        wide = h1[t].astype(F32)
        a2 = (wide * rms(wide)).astype(BF16)
        a[t] = a2
        at[t] = a2.T

    def out_copies(layer, j, s):
        copies = []
        for i, b in enumerate(blocks(j)):
            cols = pl.ds(b * LB, LB)
            copies += [
                pltpu.make_async_copy(ob.at[s, :, pl.ds(i * LB, LB)], gg_h.at[layer, :, cols], sem_o.at[s, 3 * i]),
                pltpu.make_async_copy(ob.at[s, :, pl.ds(fc + i * LB, LB)], gu_h.at[layer, :, cols], sem_o.at[s, 3 * i + 1]),
                pltpu.make_async_copy(od.at[s, pl.ds(i * LB, LB), :], gd_h.at[layer, cols, :], sem_o.at[s, 3 * i + 2]),
            ]
        return copies

    def chunk(layer, j, wgu, wdn, into_states):
        s = j % 2
        wd = jnp.concatenate([wdn[2 * j], wdn[2 * j + 1]], 0)
        wdt[...] = wd.T
        if into_states:
            wgut[...] = wgu[j].T
        pg[...] = jnp.zeros_like(pg)
        pd[...] = jnp.zeros_like(pd)

        @pl.loop(0, nt)
        def _(t):
            gu = dot(a[t], wgu[j])
            dh = dot(dy[t], wdt[...]).astype(BF16).astype(F32)
            g, u = gu[:, :fc], gu[:, fc:]
            sig = sigmoid(g)
            silu = g * sig
            hd = (silu * u).astype(BF16)
            dgu = jnp.concatenate([(dh * u * (sig + silu * (1 - sig))).astype(BF16), (dh * silu).astype(BF16)], 1)
            pg[...] += dot(at[t], dgu)
            pd[...] += dot(dyt[t], hd)
            if into_states:
                da[t] += dot(dgu, wgut[...])

        @pl.when(j >= 2)
        def _():
            for copy in out_copies(layer, j, s):
                copy.wait()

        ob[s] = pg[...].astype(BF16)
        od[s] = pd[...].T.astype(BF16)
        for copy in out_copies(layer, j, s):
            copy.start()

    @pl.loop(0, nc)
    def _(j):
        chunk(1, j, w2, w2d, True)

    @pl.loop(0, nt)
    def _(t):
        copies = (pltpu.make_async_copy(a1_h.at[t], a.at[t], sem_a.at[t]), pltpu.make_async_copy(a1t_h.at[t], at.at[t], sem_at.at[t]))
        for copy in copies:
            copy.start()
        wide = h1[t].astype(F32)
        r = rms(wide)
        da_t = da[t].astype(BF16).astype(F32)
        dn = da_t * r - wide * (r * r * r * jnp.mean(da_t * wide, -1, keepdims=True))
        dh1 = (dy[t].astype(F32) + dn).astype(BF16)
        dy[t] = dh1
        dyt[t] = dh1.T
        for copy in copies:
            copy.wait()

    for s in range(2):
        for copy in out_copies(1, s, s):
            copy.wait()

    @pl.loop(0, nc)
    def _(j):
        chunk(0, j, w1, w1d, False)

    for s in range(2):
        for copy in out_copies(0, s, s):
            copy.wait()


def gradients_of(x, dy, wg, wu, wd, n):
    tokens, d = x.shape[1:]
    layers, _, f = wg.shape
    nt, nc = tokens // TT, f // (2 * LB)
    fc = 2 * LB
    hbm = pl.BlockSpec(memory_space=pl.ANY)
    shapes = [jax.ShapeDtypeStruct(wg.shape, BF16), jax.ShapeDtypeStruct(wu.shape, BF16), jax.ShapeDtypeStruct(wd.shape, BF16),
              jax.ShapeDtypeStruct((nt, TT, d), BF16), jax.ShapeDtypeStruct((nt, d, TT), BF16)]
    v = pltpu.VMEM
    dma = pltpu.SemaphoreType.DMA
    scratch = [
        v((nc, d, 2 * fc), BF16), v((2 * nc, LB, d), BF16), v((nc, d, 2 * fc), BF16), v((2 * nc, LB, d), BF16),
        v((2 * fc, d), BF16), v((d, fc), BF16),
        v((nt, TT, d), BF16), v((nt, d, TT), BF16), v((nt, TT, d), BF16), v((nt, TT, d), BF16), v((nt, d, TT), BF16), v((nt, TT, d), F32),
        v((2, TT, d), BF16), v((TT, f), BF16), v((d, 2 * fc), F32), v((d, fc), F32), v((2, d, 2 * fc), BF16), v((2, fc, d), BF16),
        dma((2, 2)), dma((2,)), dma((nt,)), dma((nt,)), dma((nt,)), dma((2, 6)),
    ]
    return pl.pallas_call(
        functools.partial(grad_kernel, (nt, nc, n)),
        name="gradients",
        out_shape=shapes,
        in_specs=[hbm] * 5,
        out_specs=[hbm] * 5,
        scratch_shapes=scratch,
        compiler_params=pltpu.CompilerParams(vmem_limit_bytes=VMEM_LIMIT),
    )(x, dy, wg, wu, wd)[:3]


def adamw(w, m, v, g):
    m = 0.9 * m + 0.1 * g
    v = 0.95 * v + 0.05 * g * g
    step = m * lax.rsqrt(v + 1e-8) + 0.1 * w
    return (w - 0.02 * step).astype(BF16), m, v


def solution(mesh):
    n = mesh.shape["dp"]

    def step(x, dy, *arrays):
        weights, m, v = (arrays[i:i + 3] for i in (0, 3, 6))
        terms = gradients_of(x, dy, *weights, n)
        g = [lax.psum_scatter(t, "dp", scatter_dimension=1, tiled=True).astype(F32) for t in terms]
        count = sum(t.size for t in terms)
        total = lax.psum(sum(jnp.sum(t * t) for t in g), "dp")
        factor = jnp.minimum(1.0, 0.5 * lax.rsqrt(total / count + 1e-30))
        me = lax.axis_index("dp")
        new = []
        for w, mm, vv, gg in zip(weights, m, v, g, strict=True):
            rows = gg.shape[1]
            own = lax.dynamic_slice_in_dim(w, me * rows, rows, 1).astype(F32)
            wn, mn, vn = adamw(own, mm, vv, gg * factor)
            new.append((lax.all_gather(wn, "dp", axis=1, tiled=True), mn, vn))
        return tuple(one[which] for which in range(3) for one in new)

    seq, rows = P(("rep", "dp"), None, None), P(None, "dp", None)
    return jax.shard_map(
        step,
        mesh=mesh,
        in_specs=(seq, seq) + (P(),) * 3 + (rows,) * 6,
        out_specs=(P("rep"),) * 3 + (P("rep", "dp"),) * 6,
        check_vma=False,
    )
```

time: 954 us -> 613 us (0.64); the launches traced: 942 us -> 612 us
  matrix products: 377 us -> 0 us
  Pallas kernels: 0 us -> 246 us
  other arithmetic: 107 us -> 15.3 us
  waiting for transfers between devices: 217 us -> 307 us
  starting transfers between devices: 90.2 us -> 0.38 us
  local copies, waits for them, and re-layouts: 94 us -> 10.7 us
  loops' own time: 23.8 us -> 0 us
    dot_general x33 -> x0, matrix products: 377 us -> none  [the longest x11 143 us: layer(): gate = jnp.dot(a, w['w_gate'], preferred_element_type=jnp.float32)]
    pallas_call x0 -> x1, Pallas kernels: none -> 246 us  [gradients_of(): pl.pallas_call(functools.partial(grad_kernel, (nt, nc, n)), name='gradien...]
    reduce_scatter x0 -> x3, waiting for transfers between devices: none -> 156 us  [step(): lax.psum_scatter(t, 'dp', scatter_dimension=1, tiled=True).astype(F32)]
    all_gather x0 -> x3, waiting for transfers between devices: none -> 149 us  [step(): new.append((lax.all_gather(wn, 'dp', axis=1, tiled=True), mn, vn))]
    reshape x3 -> x0, waiting for transfers between devices: 149 us -> none  [step(): t.reshape(-1, *t.shape[2:])]
    dot_general x54 -> x0, starting transfers between devices: 90 us -> none  [the longest x18 33.9 us: matmul(): jnp.dot(a, w, preferred_element_type=jnp.float32).astype(jnp.bfloat16)]
    unnamed x55 -> x19, local copies, waits for them, and re-layouts: 81.6 us -> 10.7 us
    dot_general x54 -> x0, waiting for transfers between devices: 68 us -> none  [the longest x18 33.6 us: matmul(): jnp.dot(a, w, preferred_element_type=jnp.float32).astype(jnp.bfloat16)]
  transfers between devices with their start and end apart: 57 -> 6, of which waited for: 25 -> 6; matrix products, arithmetic and copies ran while one was open for 35% -> 2% of each run, Pallas kernels for 0% -> 0%
where the time goes in v1:
time: 613 us; the launch traced here: 612 us
  waiting for transfers between devices  307 us (50%)
  Pallas kernels  246 us (40%)
  between operations  16.9 us (3%)
  blocking collectives  16.1 us (3%)
  other arithmetic  15.3 us (2%)
  local copies, waits for them, and re-layouts  10.7 us (2%)
    pallas_call x1, Pallas kernels, gradients_of(): pl.pallas_call(functools.partial(grad_kernel, (nt, nc, n)), name='gradien...  246 us
    reduce_scatter x3, waiting for transfers between devices, step(): lax.psum_scatter(t, 'dp', scatter_dimension=1, tiled=True).astype(F32)  156 us
    all_gather x3, waiting for transfers between devices, step(): new.append((lax.all_gather(wn, 'dp', axis=1, tiled=True), mn, vn))  149 us
    psum x1, blocking collectives, step(): total = lax.psum(sum((jnp.sum(t * t) for t in g)), 'dp')  16.1 us
  transfers between devices with their start and end apart: 6, of which 6 were waited for; matrix products, arithmetic and copies ran while one was open for 2% of the time, Pallas kernels for 0%

profile of v1, /device:TPU:22, one launch (start us, length us, event | category | flops | bytes accessed | tf_op | source)
XLA Modules:
  0.0 611.8 jit_solution(11004464738372483686)
XLA Ops:
  7.3 245.8 %gradients.1 = (bf16[2,512,2048]{2,1,0:T(8,128)(2,1)}, bf16[2,512,2048]{2,1,0:T(8,128)(2,1)}, bf16[2,2048,512]{2,1,0:T(8,128)(2,1)}, bf16[8,512,512]{2,1,0:T(8,128)(2,1)}, bf16[8,512,512]{2,1,0:T(8,128)(2,1)}) custom-call(bf16[1,4096,512]{2,1,0:T(8,128)(2,1)} %x_h.1, bf16[1,4096,512]{2,1,0:T(8,128)(2,1)} %dy_h.1, bf16[2,512,2048]{2,1,0:T(8,128)(2,1)} %wg_h.1, ...), custom_call_target="tpu_custom_call" | custom-call | tf_op jit(solution)/shard_map/gradients/pallas_call | solution.py:188
  253.2 0.1 reduce-scatter.6.cloned.1.call-start
  253.3 0.7 reduce-scatter.6.cloned.1.call-update
  254.1 0.7 reduce-scatter.8.cloned.1.call-update
  254.8 0.1 all-gather.8.cloned.1.call-start
  254.9 54.3 %reduce-scatter.4.cloned.1.call-done = bf16[2,64,2048]{2,1,0:T(8,128)(2,1)} async-done(((bf16[2,512,2048]{2,1,0:T(8,128)(2,1)}), bf16[2,64,2048]{2,1,0:T(8,128)(2,1)}) %reduce-scatter.4.cloned.1.call-update) | async-done | bytes 524304 | tf_op jit(solution)/shard_map/reduce_scatter | solution.py:212
  309.1 2.0 fusion.9
  311.1 51.7 %reduce-scatter.6.cloned.1.call-done = bf16[2,64,2048]{2,1,0:T(8,128)(2,1)} async-done(((bf16[2,512,2048]{2,1,0:T(8,128)(2,1)}), bf16[2,64,2048]{2,1,0:T(8,128)(2,1)}) %reduce-scatter.6.cloned.1.call-update) | async-done | bytes 524304 | tf_op jit(solution)/shard_map/reduce_scatter | solution.py:212
  362.8 1.9 fusion.10
  366.0 50.5 %reduce-scatter.8.cloned.1.call-done = bf16[2,256,512]{2,1,0:T(8,128)(2,1)} async-done(((bf16[2,2048,512]{2,1,0:T(8,128)(2,1)}), bf16[2,256,512]{2,1,0:T(8,128)(2,1)}) %reduce-scatter.8.cloned.1.call-update) | async-done | bytes 524304 | tf_op jit(solution)/shard_map/reduce_scatter | solution.py:212
  416.4 1.9 fusion.11
  419.0 16.1 %psum.7 = f32[]{:T(128)} all-reduce(f32[]{:T(128)S(6)} %add.65), channel_id=1, replica_groups=mesh['rep'=8,'dp'=8] {'dp'}, use_global_device_ids=true, to_apply=%region_6.0 | all-reduce | flops 1 | bytes 8 | tf_op jit(solution)/shard_map/psum | solution.py:214
  435.8 3.0 fusion.17
  438.9 0.1 all-gather.4.cloned.1.call-start
  439.0 3.6 fusion.8
  442.7 0.1 all-gather.6.cloned.1.call-start
  442.8 2.8 fusion.14
  445.7 44.6 %all-gather.8.cloned.1.call-done = bf16[2,2048,512]{2,1,0:T(8,128)(2,1)} async-done(((bf16[2,256,512]{2,1,0:T(8,128)(2,1)}), bf16[2,2048,512]{2,1,0:T(8,128)(2,1)}) %all-gather.8.cloned.1.call-update) | async-done | bytes 4194320 | tf_op jit(solution)/shard_map/all_gather | solution.py:222
  490.3 52.0 %all-gather.4.cloned.1.call-done = bf16[2,512,2048]{2,1,0:T(8,128)(2,1)} async-done(((bf16[2,64,2048]{2,1,0:T(8,128)(2,1)}), bf16[2,512,2048]{2,1,0:T(8,128)(2,1)}) %all-gather.4.cloned.1.call-update) | async-done | bytes 4194320 | tf_op jit(solution)/shard_map/all_gather | solution.py:222
  542.3 52.0 %all-gather.6.cloned.1.call-done = bf16[2,512,2048]{2,1,0:T(8,128)(2,1)} async-done(((bf16[2,64,2048]{2,1,0:T(8,128)(2,1)}), bf16[2,512,2048]{2,1,0:T(8,128)(2,1)}) %all-gather.6.cloned.1.call-update) | async-done | bytes 4194320 | tf_op jit(solution)/shard_map/all_gather | solution.py:222
  594.3 4.9 copy.23
  599.2 2.1 copy.24
  601.4 1.6 copy-done
  602.9 2.0 copy.25
  (21 shorter events, 0.4 us)
Async XLA Ops:
  7.2 301.9 %reduce-scatter.4.cloned.1.call-start = ((), (), s32[]{:S(2)}) async-start(), calls=%async_computation.3 | async-start | bytes 4718592 | tf_op jit(solution)/shard_map/reduce_scatter | solution.py:212
  253.2 109.6 %reduce-scatter.6.cloned.1.call-start = ((), (), s32[]{:S(2)}) async-start(), calls=%async_computation.4 | async-start | bytes 4718592 | tf_op jit(solution)/shard_map/reduce_scatter | solution.py:212
  253.2 182.6 %copy-start.4 = (f32[2,256,512]{2,1,0:T(8,128)S(1)}, f32[2,256,512]{2,1,0:T(8,128)}, u32[]{:S(2)}) copy-start(f32[2,256,512]{2,1,0:T(8,128)} %param.21) | copy-start | bytes 3145732
  253.3 182.6 %copy-start.5 = (f32[2,256,512]{2,1,0:T(8,128)S(1)}, f32[2,256,512]{2,1,0:T(8,128)}, u32[]{:S(2)}) copy-start(f32[2,256,512]{2,1,0:T(8,128)} %param.18) | copy-start | bytes 3145732
  254.0 162.5 %reduce-scatter.8.cloned.1.call-start = ((), (), s32[]{:S(2)}) async-start(), calls=%async_computation.5 | async-start | bytes 4718592 | tf_op jit(solution)/shard_map/reduce_scatter | solution.py:212
  254.8 235.5 %all-gather.8.cloned.1.call-start = ((), (), s32[]{:S(2)}) async-start(), calls=%async_computation.8 | async-start | bytes 4718592 | tf_op jit(solution)/shard_map/all_gather | solution.py:222
  309.1 129.9 %copy-start.3 = (bf16[2,64,2048]{2,1,0:T(8,128)(2,1)S(1)}, bf16[2,64,2048]{2,1,0:T(8,128)(2,1)}, u32[]{:S(2)}) copy-start(bf16[2,64,2048]{2,1,0:T(8,128)(2,1)} %reduce-scatter.4.cloned.1.call-done) | copy-start | bytes 1572868
  438.8 3.9 copy-start.2
  438.9 3.9 copy-start.6
  438.9 3.9 copy-start.7
  438.9 103.4 %all-gather.4.cloned.1.call-start = ((), (), s32[]{:S(2)}) async-start(), calls=%async_computation.6 | async-start | bytes 4718592 | tf_op jit(solution)/shard_map/all_gather | solution.py:222
  442.7 151.6 %all-gather.6.cloned.1.call-start = ((), (), s32[]{:S(2)}) async-start(), calls=%async_computation.7 | async-start | bytes 4718592 | tf_op jit(solution)/shard_map/all_gather | solution.py:222
  594.3 4.9 copy-start.1
  599.2 3.7 copy-start
Sparse Core Ops, SparseCore 0:
  253.3 55.7 reduce-scatter.3
  312.0 50.7 reduce-scatter.5
  365.7 50.7 reduce-scatter.7
  439.0 51.1 all-gather.7
  492.3 49.9 all-gather.3
  544.3 49.9 all-gather.5

commit v2 on v1

v2 whole, which is shorter than its diff:
```python
import functools

import jax
import jax.numpy as jnp
from jax import lax
from jax.experimental import pallas as pl
from jax.experimental.pallas import tpu as pltpu
from jax.sharding import PartitionSpec as P

F32, BF16 = jnp.float32, jnp.bfloat16
MESH = pl.DeviceIdType.MESH
TT = 512
LB = 128
FC = 2 * LB
UNITS_HELD = 5
VMEM_LIMIT = 67_043_328


def dot(a, b):
    return jnp.dot(a, b, preferred_element_type=F32)


def rms(wide):
    return lax.rsqrt(jnp.mean(wide * wide, -1, keepdims=True) + 1e-6)


def sigmoid(g):
    return 0.5 * jnp.tanh(0.5 * g) + 0.5


def grad_kernel(nt, nc, n, x_h, dy_h, wg_h, wu_h, wd_h, og_h, ou_h, od_h, tot_h, a1_h, a1t_h,
                w1, w1d, w2, w2d, wgut, wdt, a, at, h1, dy, dyt, da, xb, hid, hd0, hd1, dgu0, dgu1,
                pg, pd, rg, rd, sg, sd, og, ou, od, ss, tots,
                sem_w, sem_x, sem_dy, sem_a, sem_at, sem_o, rg_sem, rd_sem, sg_sem, sd_sem, ts_sem, tr_sem):
    half, far = nc // 2, n // 2
    units = 2 * nc
    rows = pg.shape[1] // n
    hds, dgus = (hd0, hd1), (dgu0, dgu1)
    me = lax.axis_index("dp")
    around = [lax.rem(me + k, n) for k in range(n)]
    towards = (around[1], around[n - 1])

    barrier = pltpu.get_barrier_semaphore()
    for k in range(1, n):
        pl.semaphore_signal(barrier, inc=1, device_id={"dp": around[k]}, device_id_type=MESH)

    def block(j):
        return 2 * lax.rem(j, half) + j // half

    for layer, (wgu, wdn) in enumerate(((w1, w1d), (w2, w2d))):
        for j in range(nc):
            for s in range(2):
                cols = pl.ds((2 * (j % half) + j // half + s * nc) * LB, LB)
                pltpu.make_async_copy(wg_h.at[layer, :, cols], wgu.at[j, :, pl.ds(s * LB, LB)], sem_w.at[layer, 0]).start()
                pltpu.make_async_copy(wu_h.at[layer, :, cols], wgu.at[j, :, pl.ds(FC + s * LB, LB)], sem_w.at[layer, 0]).start()
                pltpu.make_async_copy(wd_h.at[layer, cols, :], wdn.at[j * 2 + s], sem_w.at[layer, 1]).start()

    def x_copy(t):
        s = lax.rem(t, 3)
        return pltpu.make_async_copy(x_h.at[0, pl.ds(t * TT, TT), :], xb.at[s], sem_x.at[s])

    def dy_copy(t):
        return pltpu.make_async_copy(dy_h.at[0, pl.ds(t * TT, TT), :], dy.at[t], sem_dy.at[t])

    def a_copies(t, out):
        pairs = ((a.at[t], a1_h.at[t], sem_a.at[t]), (at.at[t], a1t_h.at[t], sem_at.at[t]))
        return [pltpu.make_async_copy(*((v, h) if out else (h, v)), s) for v, h, s in pairs]

    x_copy(0).start()
    for t in range(nt):
        dy_copy(t).start()
    pltpu.make_async_copy(w1, w1, sem_w.at[0, 0]).wait()
    pltpu.make_async_copy(w1d, w1d, sem_w.at[0, 1]).wait()
    ss[...] = jnp.zeros_like(ss)

    def forward_back(t):
        y = dot(hid[...], w1d[...].reshape(2 * nc * LB, -1))
        h1[t] = (xb[lax.rem(t, 3)].astype(F32) + y.astype(BF16).astype(F32)).astype(BF16)
        da[t] = jnp.zeros(da.shape[1:], F32)
        dyt[t] = dy[t].T

    @pl.loop(0, nt)
    def _(t):
        before = jnp.maximum(t - 1, 0)
        x_copy(t).wait()
        dy_copy(t).wait()

        @pl.when(t + 1 < nt)
        def _():
            x_copy(t + 1).start()

        forward_back(before)
        wide = xb[lax.rem(t, 3)].astype(F32)
        a1 = (wide * rms(wide)).astype(BF16)
        a[t] = a1
        at[t] = a1.T
        for j in range(nc):
            gu = dot(a1, w1[j])
            g, u = gu[:, :FC], gu[:, FC:]
            hid[:, j * FC:(j + 1) * FC] = (g * sigmoid(g) * u).astype(BF16)
        for copy in a_copies(t, True):
            copy.start()

    forward_back(nt - 1)
    pltpu.make_async_copy(w2, w2, sem_w.at[1, 0]).wait()
    pltpu.make_async_copy(w2d, w2d, sem_w.at[1, 1]).wait()

    @pl.loop(0, nt)
    def _(t):
        for copy in a_copies(t, True):
            copy.wait()
        wide = h1[t].astype(F32)
        a2 = (wide * rms(wide)).astype(BF16)
        a[t] = a2
        at[t] = a2.T

    def g_copy(u, s, way, both):
        part = (lambda ref: ref) if both else (lambda ref: ref.at[way])
        return pltpu.make_async_remote_copy(
            part(sg.at[way, s]), part(rg.at[way, lax.rem(u, 2), s]), sg_sem.at[way, s], rg_sem.at[way, lax.rem(u, 2), s],
            device_id={"dp": towards[way]}, device_id_type=MESH)

    def d_copy(j, way, both):
        k = lax.rem(j, far)
        part = (lambda ref: ref) if both else (lambda ref: ref.at[way])
        return pltpu.make_async_remote_copy(
            part(sd.at[way, k]), part(rd.at[way, k]), sd_sem.at[way, k], rd_sem.at[way, k],
            device_id={"dp": towards[way]}, device_id_type=MESH)

    def relay(u, s):
        j, slot, old = lax.rem(u, nc), lax.rem(u, UNITS_HELD), lax.rem(u, 2)
        for way in range(2):
            e = around[far - s] if way == 0 else around[n - far + s]

            @pl.when(u > 0)
            def _():
                g_copy(u - 1, s, way, s > 0).wait_send()

            if s > 0:
                g_copy(u, s - 1, way, s > 1).wait_recv()
            for h in range(2):
                if s == 0 and h != way:
                    continue
                own = pg[slot, pl.ds(pl.multiple_of(e * rows, rows), rows), h * FC:(h + 1) * FC]
                if s > 1 or (s == 1 and h == way):
                    own += rg[way, old, s - 1, h].astype(F32)
                sg[way, s, h] = own.astype(BF16)
            g_copy(u, s, way, s > 0).start()

            @pl.when(lax.rem(e, far) == lax.rem(j, far))
            def _():
                k = lax.rem(j, far)

                @pl.when(u >= far)
                def _():
                    d_copy(j, way, s > 0).wait_send()

                if s > 0:
                    d_copy(j, way, s > 1).wait_recv()
                tall = pd.shape[2] // 2
                for h in range(2):
                    if s == 0 and h != way:
                        continue
                    own = pd[slot, e // far, h * tall:(h + 1) * tall, :]
                    if s > 1 or (s == 1 and h == way):
                        own += rd[way, k, h].astype(F32)
                    sd[way, k, h] = own.astype(BF16)
                d_copy(j, way, s > 0).start()

    def square(g):
        wide = g.astype(F32)
        ss[...] += jnp.sum((wide * wide).reshape(-1, *ss.shape), 0)

    def arrive(u):
        j, slot, old, layer = lax.rem(u, nc), lax.rem(u, UNITS_HELD), lax.rem(u, 2), 1 - u // nc
        k = lax.rem(j, far)
        for way in range(2):
            g_copy(u, far - 1, way, True).wait_recv()
        for h, out in enumerate((og, ou)):
            own = pg[slot, pl.ds(pl.multiple_of(me * rows, rows), rows), h * FC:(h + 1) * FC]
            own = (own + rg[0, old, far - 1, h].astype(F32) + rg[1, old, far - 1, h].astype(F32)).astype(BF16)
            for s in range(2):
                piece = own[:, s * LB:(s + 1) * LB]
                out[layer, :, pl.ds(pl.multiple_of((block(j) + s * nc) * LB, LB), LB)] = piece
                square(piece)

        @pl.when(lax.rem(me, far) == k)
        def _():
            tall = pd.shape[2] // 2
            for way in range(2):
                d_copy(j, way, True).wait_recv()
            for h in range(2):
                own = pd[slot, me // far, h * tall:(h + 1) * tall, :]
                own = own + rd[0, k, h].astype(F32) + rd[1, k, h].astype(F32)
                own = own.T.astype(BF16)
                od[layer, pl.ds(pl.multiple_of(j // half * LB, LB), LB), h * tall:(h + 1) * tall] = own
                for s in range(tall // LB):
                    square(own[:, s * LB:(s + 1) * LB])

    def turn_round(at_step):
        p, q = at_step // far, lax.rem(at_step, far)

        @pl.when((q == 0) & (p >= 4) & (p < units + 4))
        def _():
            arrive(p - 4)

        for when, s, lag in ((0, 0, 1), (1, 3, 3), (2, 2, 2), (3, 1, 1)):
            @pl.when((q == when) & (p >= lag) & (p < units + lag))
            def _(s=s, lag=lag):
                relay(p - lag, s)

    def front(j, t, wgu, slot):
        gu = dot(a[t], wgu[j])
        dh = dot(dy[t], wdt[lax.rem(j, 2)]).astype(BF16).astype(F32)
        g, u = gu[:, :FC], gu[:, FC:]
        sig = sigmoid(g)
        silu = g * sig
        hds[slot][...] = (silu * u).astype(BF16)
        dgus[slot][:, :FC] = (dh * u * (sig + silu * (1 - sig))).astype(BF16)
        dgus[slot][:, FC:] = (dh * silu).astype(BF16)

    def back(u, t, slot, into_states, first=None):
        p, k = lax.rem(u, 2), lax.rem(u, UNITS_HELD)
        keep = (lambda old: old) if first is None else (lambda old: jnp.where(first, jnp.zeros_like(old), old))
        pg[k] = keep(pg[k]) + dot(at[t], dgus[slot][...])
        hd = dot(dyt[t], hds[slot][...])
        for s in range(2):
            pd[k, s] = keep(pd[k, s]) + hd[:, s * LB:(s + 1) * LB]
        if into_states:
            da[t] += dot(dgus[slot][...], wgut[p])

    def turn(j, t, wgu, wdn, into_states):
        p = lax.rem(j, 2)
        if into_states:
            i = pl.multiple_of(lax.rem(t, 4) * LB, LB)
            wgut[p, :, pl.ds(i, LB)] = wgu[j, pl.ds(i, LB), :].T
        s = lax.rem(t, 2)
        wdt[p, :, pl.ds(pl.multiple_of(s * LB, LB), LB)] = wdn[2 * j + s].T

    def layer_back(start, wgu, wdn, into_states):
        for t in range(4):
            turn(0, t, wgu, wdn, into_states)
        for h, g in zip(hds, dgus):
            h[...] = jnp.zeros_like(h)
            g[...] = jnp.zeros_like(g)

        @pl.loop(0, nc * nt // 2)
        def _(i):
            j, t = i // (nt // 2), 2 * lax.rem(i, nt // 2)
            k = jnp.maximum(2 * i - 1, 0)
            jn = jnp.minimum(j + 1, nc - 1)
            front(j, t, wgu, 0)
            back(start + k // nt, lax.rem(k, nt), 1, into_states)
            turn(jn, t, wgu, wdn, into_states)
            turn(jn, t + 1, wgu, wdn, into_states)
            front(j, t + 1, wgu, 1)
            back(start + j, t, 0, into_states, t == 0)
            turn_round(start * (nt // 2) + i)

        back(start + nc - 1, nt - 1, 1, into_states)

    pl.semaphore_wait(barrier, n - 1)
    layer_back(0, w2, w2d, True)

    for t in range(nt):
        for copy in a_copies(t, False):
            copy.start()

    @pl.loop(0, nt)
    def _(t):
        wide = h1[t].astype(F32)
        r = rms(wide)
        da_t = da[t].astype(BF16).astype(F32)
        dn = da_t * r - wide * (r * r * r * jnp.mean(da_t * wide, -1, keepdims=True))
        dh1 = (dy[t].astype(F32) + dn).astype(BF16)
        dy[t] = dh1
        dyt[t] = dh1.T
        for copy in a_copies(t, False):
            copy.wait()

    layer_back(nc, w1, w1d, False)

    @pl.loop(units * far, (units + 3) * far + 1)
    def _(at_step):
        turn_round(at_step)

    for way in range(2):
        for s in range(far):
            g_copy(units - 1, s, way, s > 0).wait_send()
            e = around[far - s] if way == 0 else around[n - far + s]
            d_copy(lax.rem(e, far), way, s > 0).wait_send()

    tots[pl.ds(me, 1)] = ss[...][None]
    copies = [
        pltpu.make_async_remote_copy(ss, tots.at[me], ts_sem.at[k], tr_sem.at[n - k], device_id={"dp": around[k]}, device_id_type=MESH)
        for k in range(1, n)
    ]
    for copy in copies:
        copy.start()
    outs = [pltpu.make_async_copy(*pair, sem_o.at[i]) for i, pair in enumerate(((og, og_h), (ou, ou_h), (od, od_h)))]
    for copy in outs:
        copy.start()
    for copy in copies:
        copy.wait_send()
    for k in range(1, n):
        pltpu.make_async_remote_copy(ss, tots.at[around[k]], ts_sem.at[k], tr_sem.at[k], device_id={"dp": around[k]}, device_id_type=MESH).wait_recv()
    last = pltpu.make_async_copy(tots, tot_h, sem_o.at[3])
    last.start()
    for copy in (*outs, last):
        copy.wait()


def gradients_of(x, dy, wg, wu, wd, n):
    tokens, d = x.shape[1:]
    layers, _, f = wg.shape
    nt, nc = tokens // TT, f // FC
    far = n // 2
    hbm = pl.BlockSpec(memory_space=pl.ANY)
    shape = jax.ShapeDtypeStruct
    shapes = [shape((layers, d // n, f), BF16), shape((layers, d // n, f), BF16), shape((layers, f // n, d), BF16), shape((n, 8, LB), F32),
              shape((nt, TT, d), BF16), shape((nt, d, TT), BF16)]
    v = pltpu.VMEM
    dma = pltpu.SemaphoreType.DMA
    rows = d // n
    scratch = [
        v((nc, d, 2 * FC), BF16), v((2 * nc, LB, d), BF16), v((nc, d, 2 * FC), BF16), v((2 * nc, LB, d), BF16),
        v((2, 2 * FC, d), BF16), v((2, d, FC), BF16),
        v((nt, TT, d), BF16), v((nt, d, TT), BF16), v((nt, TT, d), BF16), v((nt, TT, d), BF16), v((nt, d, TT), BF16), v((nt, TT, d), F32),
        v((3, TT, d), BF16), v((TT, f), BF16), v((TT, FC), BF16), v((TT, FC), BF16), v((TT, 2 * FC), BF16), v((TT, 2 * FC), BF16),
        v((UNITS_HELD, d, 2 * FC), F32), v((UNITS_HELD, 2, d, LB), F32),
        v((2, 2, far, 2, rows, FC), BF16), v((2, far, 2, d // 2, LB), BF16), v((2, far, 2, rows, FC), BF16), v((2, far, 2, d // 2, LB), BF16),
        v((layers, rows, f), BF16), v((layers, rows, f), BF16), v((layers, f // n, d), BF16), v((8, LB), F32), v((n, 8, LB), F32),
        dma((2, 2)), dma((3,)), dma((nt,)), dma((nt,)), dma((nt,)), dma((4,)),
        dma((2, 2, far)), dma((2, far)), dma((2, far)), dma((2, far)), dma((n,)), dma((n,)),
    ]
    return pl.pallas_call(
        functools.partial(grad_kernel, nt, nc, n),
        name="gradients",
        out_shape=shapes,
        in_specs=[hbm] * 5,
        out_specs=[hbm] * len(shapes),
        scratch_shapes=scratch,
        compiler_params=pltpu.CompilerParams(vmem_limit_bytes=VMEM_LIMIT, collective_id=0, has_side_effects=True),
    )(x, dy, wg, wu, wd)[:4]


def adamw(w, m, v, g):
    m = 0.9 * m + 0.1 * g
    v = 0.95 * v + 0.05 * g * g
    step = m * lax.rsqrt(v + 1e-8) + 0.1 * w
    return (w - 0.02 * step).astype(BF16), m, v


def solution(mesh):
    n = mesh.shape["dp"]

    def step(x, dy, *arrays):
        weights, m, v = (arrays[i:i + 3] for i in (0, 3, 6))
        *g, squares = gradients_of(x, dy, *weights, n)
        count = sum(w.size for w in weights)
        factor = jnp.minimum(1.0, 0.5 * lax.rsqrt(jnp.sum(squares) / count + 1e-30))
        me = lax.axis_index("dp")
        new = []
        for w, mm, vv, gg in zip(weights, m, v, g, strict=True):
            rows = gg.shape[1]
            own = lax.dynamic_slice_in_dim(w, me * rows, rows, 1).astype(F32)
            wn, mn, vn = adamw(own, mm, vv, gg.astype(F32) * factor)
            new.append((lax.all_gather(wn, "dp", axis=1, tiled=True), mn, vn))
        return tuple(one[which] for which in range(3) for one in new)

    seq, rows = P(("rep", "dp"), None, None), P(None, "dp", None)
    return jax.shard_map(
        step,
        mesh=mesh,
        in_specs=(seq, seq) + (P(),) * 3 + (rows,) * 6,
        out_specs=(P("rep"),) * 3 + (P("rep", "dp"),) * 6,
        check_vma=False,
    )
```

time: 613 us -> 427 us (0.70)
  waiting for transfers between devices: 307 us -> 148 us
  blocking collectives: 16.1 us -> 0 us
    reduce_scatter x3 -> x0, waiting for transfers between devices: 156 us -> none  [step(): lax.psum_scatter(t, 'dp', scatter_dimension=1, tiled=True).astype(F32)]
    psum x1 -> x0, blocking collectives: 16.1 us -> none  [step(): total = lax.psum(sum((jnp.sum(t * t) for t in g)), 'dp')]
  transfers between devices with their start and end apart: 6 -> 3, of which waited for: 6 -> 3; matrix products, arithmetic and copies ran while one was open for 2% -> 2% of each run, Pallas kernels for 0% -> 0%
where the time goes in v2:
time: 427 us
  Pallas kernels  242 us (57%)
  waiting for transfers between devices  148 us (35%)
  between operations  14.5 us (3%)
  other arithmetic  11.6 us (3%)
  local copies, waits for them, and re-layouts  10.7 us (3%)
    pallas_call x1, Pallas kernels, gradients_of(): pl.pallas_call(functools.partial(grad_kernel, nt, nc, n), name='gradients...  242 us
    all_gather x3, waiting for transfers between devices, step(): new.append((lax.all_gather(wn, 'dp', axis=1, tiled=True), mn, vn))  147 us
    unnamed x13, local copies, waits for them, and re-layouts  10.7 us
    convert_element_type x3, other arithmetic, adamw(): return ((w - 0.02 * step).astype(BF16), m, v)  10.1 us
  transfers between devices with their start and end apart: 3, of which 3 were waited for; matrix products, arithmetic and copies ran while one was open for 2% of the time, Pallas kernels for 0%

profile of v2, /device:TPU:22, one launch (start us, length us, event | category | flops | bytes accessed | tf_op | source)
XLA Modules:
  0.0 426.6 jit_solution(14242952821758713236)
XLA Ops:
  7.2 0.1 all-gather.4.cloned.1.call-start
  7.3 242.1 %gradients.1 = (bf16[2,64,2048]{2,1,0:T(8,128)(2,1)}, bf16[2,64,2048]{2,1,0:T(8,128)(2,1)}, bf16[2,256,512]{2,1,0:T(8,128)(2,1)}, f32[8,8,128]{2,1,0:T(8,128)}, ...) custom-call(bf16[1,4096,512]{2,1,0:T(8,128)(2,1)} %x_h.1, bf16[1,4096,512]{2,1,0:T(8,128)(2,1)} %dy_h.1, ...), custom_call_target="tpu_custom_call" | custom-call | tf_op jit(solution)/shard_map/gradients/pallas_call | solution.py:336
  249.3 0.0 copy-start.2
  249.4 0.0 copy-start.3
  249.4 1.5 reduce_sum.9
  251.6 3.7 fusion.2
  255.2 0.1 all-gather.4.cloned.1.call-update
  255.3 0.1 all-gather.8.cloned.1.call-start
  255.4 0.0 copy-done.2
  255.4 0.0 copy-done.3
  255.4 3.1 fusion.8
  258.5 0.1 all-gather.8.cloned.1.call-update
  258.6 0.1 all-gather.6.cloned.1.call-start
  258.6 0.0 copy-done.4
  258.6 3.3 fusion.5
  262.0 0.1 all-gather.6.cloned.1.call-update
  262.0 43.1 %all-gather.4.cloned.1.call-done = bf16[2,512,2048]{2,1,0:T(8,128)(2,1)} async-done(((bf16[2,64,2048]{2,1,0:T(8,128)(2,1)}), bf16[2,512,2048]{2,1,0:T(8,128)(2,1)}) %all-gather.4.cloned.1.call-update) | async-done | bytes 4194320 | tf_op jit(solution)/shard_map/all_gather | solution.py:368
  305.1 52.1 %all-gather.8.cloned.1.call-done = bf16[2,2048,512]{2,1,0:T(8,128)(2,1)} async-done(((bf16[2,256,512]{2,1,0:T(8,128)(2,1)}), bf16[2,2048,512]{2,1,0:T(8,128)(2,1)}) %all-gather.8.cloned.1.call-update) | async-done | bytes 4194320 | tf_op jit(solution)/shard_map/all_gather | solution.py:368
  357.2 52.2 %all-gather.6.cloned.1.call-done = bf16[2,512,2048]{2,1,0:T(8,128)(2,1)} async-done(((bf16[2,64,2048]{2,1,0:T(8,128)(2,1)}), bf16[2,512,2048]{2,1,0:T(8,128)(2,1)}) %all-gather.6.cloned.1.call-update) | async-done | bytes 4194320 | tf_op jit(solution)/shard_map/all_gather | solution.py:368
  409.4 4.9 %copy.23 = bf16[2,512,2048]{2,1,0:T(8,128)(2,1)} copy(bf16[2,512,2048]{2,1,0:T(8,128)(2,1)} %all-gather.4.cloned.1.call-done) | data formatting | bytes 8388608
  414.3 0.0 copy-done.1
  414.3 2.1 copy.24
  416.5 1.6 copy-done
  418.0 2.0 copy.25
  (3 shorter events, 0.0 us)
Async XLA Ops:
  7.2 297.9 %all-gather.4.cloned.1.call-start = ((), (), s32[]{:S(2)}) async-start(), calls=%async_computation | async-start | bytes 4718592 | tf_op jit(solution)/shard_map/all_gather | solution.py:368
  249.3 6.0 %copy-start.2 = (f32[2,256,512]{2,1,0:T(8,128)S(1)}, f32[2,256,512]{2,1,0:T(8,128)}, u32[]{:S(2)}) copy-start(f32[2,256,512]{2,1,0:T(8,128)} %param.21) | copy-start | bytes 3145732
  249.4 6.0 %copy-start.3 = (f32[2,256,512]{2,1,0:T(8,128)S(1)}, f32[2,256,512]{2,1,0:T(8,128)}, u32[]{:S(2)}) copy-start(f32[2,256,512]{2,1,0:T(8,128)} %param.18) | copy-start | bytes 3145732
  255.2 3.4 copy-start.4
  255.3 101.9 %all-gather.8.cloned.1.call-start = ((), (), s32[]{:S(2)}) async-start(), calls=%async_computation.2 | async-start | bytes 4718592 | tf_op jit(solution)/shard_map/all_gather | solution.py:368
  258.6 150.8 %all-gather.6.cloned.1.call-start = ((), (), s32[]{:S(2)}) async-start(), calls=%async_computation.1 | async-start | bytes 4718592 | tf_op jit(solution)/shard_map/all_gather | solution.py:368
  409.4 4.9 %copy-start.1 = (bf16[2,512,2048]{2,1,0:T(8,128)(2,1)S(1)}, bf16[2,512,2048]{2,1,0:T(8,128)(2,1)}, u32[]{:S(2)}) copy-start(bf16[2,512,2048]{2,1,0:T(8,128)(2,1)} %all-gather.6.cloned.1.call-done) | copy-start | bytes 12582916
  414.3 3.7 copy-start
Sparse Core Ops, SparseCore 0:
  255.4 49.6 all-gather.3
  307.3 49.9 all-gather.7
  359.4 49.9 all-gather.5

commit v3 on v2

--- a/solution.py
+++ b/solution.py
@@ -344,11 +344,133 @@
     )(x, dy, wg, wu, wd)[:4]
 
 
-def adamw(w, m, v, g):
-    m = 0.9 * m + 0.1 * g
-    v = 0.95 * v + 0.05 * g * g
-    step = m * lax.rsqrt(v + 1e-8) + 0.1 * w
-    return (w - 0.02 * step).astype(BF16), m, v
+def update_kernel(n, count, *refs):
+    gs, tot_h, ws, ms, vs = refs[:3], refs[3], refs[4:7], refs[7:10], refs[10:13]
+    ow, om, ov = refs[13:16], refs[16:19], refs[19:22]
+    full, gb, mb, vb = refs[22:25], refs[25:28], refs[28:31], refs[31:34]
+    tots, in_sem, tot_sem, mv_sem, w_sem, send_sem, recv_sem = refs[34:]
+    far = n // 2
+    layers = full[0].shape[0]
+    me = lax.axis_index("dp")
+    around = [lax.rem(me + k, n) for k in range(n)]
+    towards = (around[1], around[n - 1])
+    pieces = [(i, layer) for layer in range(layers) for i in range(3)]
+
+    barrier = pltpu.get_barrier_semaphore()
+    for other in towards:
+        pl.semaphore_signal(barrier, inc=1, device_id={"dp": other}, device_id_type=MESH)
+
+    def block(i, origin, half=None):
+        rows = full[i].shape[1] // n
+        start = origin * rows
+        if half is not None:
+            rows //= 2
+            start += half * rows
+        return pl.ds(pl.multiple_of(start, rows), rows)
+
+    loads = {}
+    total = pltpu.make_async_copy(tot_h, tots, tot_sem)
+    total.start()
+    for k, (i, layer) in enumerate(pieces):
+        own = block(i, me)
+        loads[k] = [
+            pltpu.make_async_copy(src, dst, in_sem.at[k, c])
+            for c, (src, dst) in enumerate((
+                (gs[i].at[layer], gb[i].at[layer]), (ws[i].at[layer, own, :], full[i].at[layer, own, :]),
+                (ms[i].at[layer], mb[i].at[layer]), (vs[i].at[layer], vb[i].at[layer])))
+        ]
+        for copy in loads[k]:
+            copy.start()
+    total.wait()
+    factor = jnp.minimum(1.0, 0.5 * lax.rsqrt(jnp.sum(tots[...], keepdims=True).reshape(1, 1) / count + 1e-30))
+
+    def pass_on(k, s, way):
+        i, layer = pieces[k]
+        origin = around[(n - s) % n] if way == 0 else around[s]
+        rows = block(i, origin, way if s == far - 1 else None)
+        return pltpu.make_async_remote_copy(
+            full[i].at[layer, rows, :], full[i].at[layer, rows, :], send_sem.at[way, s, k], recv_sem.at[way, s, k],
+            device_id={"dp": towards[way]}, device_id_type=MESH)
+
+    def came(k, s, way):
+        i, layer = pieces[k]
+        origin = around[n - s - 1] if way == 0 else around[s + 1]
+        rows = block(i, origin, way if s == far - 1 else None)
+        here = full[i].at[layer, rows, :]
+        return pltpu.make_async_remote_copy(
+            here, here, send_sem.at[way, s, k], recv_sem.at[way, s, k], device_id={"dp": towards[way]}, device_id_type=MESH
+        ), pltpu.make_async_copy(here, ow[i].at[layer, rows, :], w_sem.at[way, s, k])
+
+    outs = []
+    for k, (i, layer) in enumerate(pieces):
+        for copy in loads[k]:
+            copy.wait()
+        rows = mb[i].shape[1]
+        some = max(16, rows // 8)
+        first = me * rows
+
+        @pl.loop(0, rows // some)
+        def _(r):
+            here = pl.ds(pl.multiple_of(r * some, some), some)
+            there = pl.ds(pl.multiple_of(first + r * some, some), some)
+            g = gb[i][layer, here, :].astype(F32) * factor
+            m = 0.9 * mb[i][layer, here, :] + 0.1 * g
+            v = 0.95 * vb[i][layer, here, :] + 0.05 * g * g
+            w = full[i][layer, there, :].astype(F32)
+            step = m * lax.rsqrt(v + 1e-8) + 0.1 * w
+            mb[i][layer, here, :] = m
+            vb[i][layer, here, :] = v
+            full[i][layer, there, :] = (w - 0.02 * step).astype(BF16)
+
+        if k == 0:
+            pl.semaphore_wait(barrier, 2)
+        for way in range(2):
+            pass_on(k, 0, way).start()
+        own = block(i, me)
+        outs += [
+            pltpu.make_async_copy(mb[i].at[layer], om[i].at[layer], mv_sem.at[k, 0]),
+            pltpu.make_async_copy(vb[i].at[layer], ov[i].at[layer], mv_sem.at[k, 1]),
+            pltpu.make_async_copy(full[i].at[layer, own, :], ow[i].at[layer, own, :], mv_sem.at[k, 2]),
+        ]
+        for copy in outs[-3:]:
+            copy.start()
+
+    for s in range(far):
+        for k in range(len(pieces)):
+            for way in range(2):
+                arrival, out = came(k, s, way)
+                arrival.wait_recv()
+                if s + 1 < far:
+                    pass_on(k, s + 1, way).start()
+                out.start()
+                outs.append(out)
+    for s in range(far):
+        for k in range(len(pieces)):
+            for way in range(2):
+                pass_on(k, s, way).wait_send()
+    for copy in outs:
+        copy.wait()
+
+
+def update(g, squares, w, m, v, n):
+    hbm = pl.BlockSpec(memory_space=pl.ANY)
+    shape = lambda like: jax.ShapeDtypeStruct(like.shape, like.dtype)
+    dma = pltpu.SemaphoreType.DMA
+    far, pieces = n // 2, 3 * w[0].shape[0]
+    scratch = [pltpu.VMEM(like.shape, like.dtype) for group in (w, g, m, v) for like in group] + [
+        pltpu.VMEM(squares.shape, F32), dma((pieces, 4)), dma, dma((pieces, 3)),
+        dma((2, far, pieces)), dma((2, far, pieces)), dma((2, far, pieces)),
+    ]
+    out = pl.pallas_call(
+        functools.partial(update_kernel, n, sum(one.size for one in w)),
+        name="update",
+        out_shape=[shape(like) for group in (w, m, v) for like in group],
+        in_specs=[hbm] * 13,
+        out_specs=[hbm] * 9,
+        scratch_shapes=scratch,
+        compiler_params=pltpu.CompilerParams(vmem_limit_bytes=VMEM_LIMIT, collective_id=1, has_side_effects=True),
+    )(*g, squares, *w, *m, *v)
+    return tuple(out)
 
 
 def solution(mesh):
@@ -357,16 +479,7 @@
     def step(x, dy, *arrays):
         weights, m, v = (arrays[i:i + 3] for i in (0, 3, 6))
         *g, squares = gradients_of(x, dy, *weights, n)
-        count = sum(w.size for w in weights)
-        factor = jnp.minimum(1.0, 0.5 * lax.rsqrt(jnp.sum(squares) / count + 1e-30))
-        me = lax.axis_index("dp")
-        new = []
-        for w, mm, vv, gg in zip(weights, m, v, g, strict=True):
-            rows = gg.shape[1]
-            own = lax.dynamic_slice_in_dim(w, me * rows, rows, 1).astype(F32)
-            wn, mn, vn = adamw(own, mm, vv, gg.astype(F32) * factor)
-            new.append((lax.all_gather(wn, "dp", axis=1, tiled=True), mn, vn))
-        return tuple(one[which] for which in range(3) for one in new)
+        return update(g, squares, weights, m, v, n)
 
     seq, rows = P(("rep", "dp"), None, None), P(None, "dp", None)
     return jax.shard_map(

time: 427 us -> 377 us (0.88)
  waiting for transfers between devices: 148 us -> 0 us
  Pallas kernels: 242 us -> 359 us
  between operations: 14.5 us -> 0.68 us
  other arithmetic: 11.6 us -> 0 us
  local copies, waits for them, and re-layouts: 10.7 us -> 16.6 us
    all_gather x3 -> x0, waiting for transfers between devices: 147 us -> none  [step(): new.append((lax.all_gather(wn, 'dp', axis=1, tiled=True), mn, vn))]
    pallas_call x0 -> x1, Pallas kernels: none -> 117 us  [update(): pl.pallas_call(functools.partial(update_kernel, n, sum((one.size for one...]
    convert_element_type x3 -> x0, other arithmetic: 10.1 us -> none  [adamw(): return ((w - 0.02 * step).astype(BF16), m, v)]
    unnamed x13 -> x25, local copies, waits for them, and re-layouts: 10.7 us -> 16.6 us
  transfers between devices with their start and end apart: 3 -> 0, of which waited for: 3 -> 0; matrix products, arithmetic and copies ran while one was open for 2% -> 0% of each run, Pallas kernels for 0% -> 0%
where the time goes in v3:
time: 377 us
  Pallas kernels  359 us (95%)
  local copies, waits for them, and re-layouts  16.6 us (4%)
    pallas_call x1, Pallas kernels, gradients_of(): pl.pallas_call(functools.partial(grad_kernel, nt, nc, n), name='gradients...  242 us
    pallas_call x1, Pallas kernels, update(): pl.pallas_call(functools.partial(update_kernel, n, sum((one.size for one...  117 us
    unnamed x25, local copies, waits for them, and re-layouts  16.6 us

profile of v3, /device:TPU:22, one launch (start us, length us, event | category | flops | bytes accessed | tf_op | source)
XLA Modules:
  0.0 376.5 jit_solution(14648218305629186421)
XLA Ops:
  0.6 242.1 %gradients.1 = (bf16[2,64,2048]{2,1,0:T(8,128)(2,1)}, bf16[2,64,2048]{2,1,0:T(8,128)(2,1)}, bf16[2,256,512]{2,1,0:T(8,128)(2,1)}, f32[8,8,128]{2,1,0:T(8,128)}, ...) custom-call(bf16[1,4096,512]{2,1,0:T(8,128)(2,1)} %x_h.1, bf16[1,4096,512]{2,1,0:T(8,128)(2,1)} %dy_h.1, ...), custom_call_target="tpu_custom_call" | custom-call | tf_op jit(solution)/shard_map/gradients/pallas_call | solution.py:336
  242.7 117.2 %update.1 = (bf16[2,512,2048]{2,1,0:T(8,128)(2,1)}, bf16[2,512,2048]{2,1,0:T(8,128)(2,1)}, bf16[2,2048,512]{2,1,0:T(8,128)(2,1)}, f32[2,64,2048]{2,1,0:T(8,128)}...) custom-call(bf16[2,64,2048]{2,1,0:T(8,128)(2,1)} %get-tuple-element., ...), custom_call_target="tpu_custom_call" | custom-call | tf_op jit(solution)/shard_map/update/pallas_call | solution.py:464
  359.9 0.0 copy-start.1
  359.9 4.9 %copy.29 = bf16[2,512,2048]{2,1,0:T(8,128)(2,1)} copy(bf16[2,512,2048]{2,1,0:T(8,128)(2,1)} %get-tuple-element.26) | data formatting | bytes 8388608
  364.8 0.0 copy-done.1
  364.8 0.0 copy-start
  364.8 2.1 copy.30
  367.0 1.6 copy-done
  368.5 0.0 copy-start.7
  368.6 0.0 copy-start.6
  368.6 2.1 copy.31
  370.7 0.0 copy-done.7
  370.7 0.0 copy-start.5
  370.7 1.0 copy.32
  371.7 0.0 copy-done.6
  371.7 1.0 copy.33
  372.6 0.0 copy-done.5
  372.6 1.0 copy.34
  373.6 0.0 copy-done.4
  373.6 1.0 copy.35
  374.6 0.0 copy-done.3
  374.6 1.0 copy.36
  375.6 0.0 copy-done.2
  375.6 1.0 copy.37
  (3 shorter events, 0.0 us)
Async XLA Ops:
  359.9 5.0 %copy-start.1 = (bf16[2,512,2048]{2,1,0:T(8,128)(2,1)S(1)}, bf16[2,512,2048]{2,1,0:T(8,128)(2,1)}, u32[]{:S(2)}) copy-start(bf16[2,512,2048]{2,1,0:T(8,128)(2,1)} %get-tuple-element.27) | copy-start | bytes 12582916
  364.8 3.7 copy-start
  368.5 2.1 copy-start.7
  368.6 3.1 copy-start.6
  370.7 2.0 copy-start.5
  370.7 2.9 copy-start.4
  370.7 3.9 %copy-start.3 = (f32[2,64,2048]{2,1,0:T(8,128)S(1)}, f32[2,64,2048]{2,1,0:T(8,128)}, u32[]{:S(2)}) copy-start(f32[2,64,2048]{2,1,0:T(8,128)} %get-tuple-element.33) | copy-start | bytes 3145732
  371.7 3.9 %copy-start.2 = (f32[2,256,512]{2,1,0:T(8,128)S(1)}, f32[2,256,512]{2,1,0:T(8,128)}, u32[]{:S(2)}) copy-start(f32[2,256,512]{2,1,0:T(8,128)} %get-tuple-element.34) | copy-start | bytes 3145732

commit v4 on v2

v4 whole, which is shorter than its diff:
```python
import functools

import jax
import jax.numpy as jnp
from jax import lax
from jax.experimental import pallas as pl
from jax.experimental.pallas import tpu as pltpu
from jax.sharding import PartitionSpec as P

F32, BF16 = jnp.float32, jnp.bfloat16
MESH = pl.DeviceIdType.MESH
TT = 512
LB = 128
FC = 2 * LB
UNITS_HELD = 5
VMEM_BYTES = 67_043_328


def dot(a, b):
    return jnp.dot(a, b, preferred_element_type=F32)


def rms(wide):
    return lax.rsqrt(jnp.mean(wide * wide, -1, keepdims=True) + 1e-6)


def sigmoid(g):
    return 0.5 * jnp.tanh(0.5 * g) + 0.5


def step_kernel(nt, nc, n, count, x_h, dy_h, wg_h, wu_h, wd_h, mg_h, mu_h, md_h, vg_h, vu_h, vd_h,
                fg, fu, fd, wide_ref, gu_h, a1t_h,
                wgut, wdt, a, at, h1, dy, dyt, xb, hid, hd0, hd1, dgu0, dgu1,
                pg, pd, rg, rd, sg, sd, og, ou, od, ss, tots,
                sem_w, sem_x, sem_dy, sem_at, sem_gu, rg_sem, rd_sem, sg_sem, sd_sem, ts_sem, tr_sem, mv_sem, ag_send, ag_recv):
    half, far = nc // 2, n // 2
    units = 2 * nc
    rows = pg.shape[1] // n
    hds, dgus = (hd0, hd1), (dgu0, dgu1)
    full, own_g = (fg, fu, fd), (og, ou, od)
    da = wide_ref
    me = lax.axis_index("dp")
    around = [lax.rem(me + k, n) for k in range(n)]
    towards = (around[1], around[n - 1])

    barrier = pltpu.get_barrier_semaphore()
    for k in range(1, n):
        pl.semaphore_signal(barrier, inc=1, device_id={"dp": around[k]}, device_id_type=MESH)

    def block(j):
        return 2 * lax.rem(j, half) + j // half

    def at_block(b):
        return pl.ds(b * LB if isinstance(b, int) else pl.multiple_of(b * LB, LB), LB)

    def x_copy(t):
        s = lax.rem(t, 3)
        return pltpu.make_async_copy(x_h.at[0, pl.ds(t * TT, TT), :], xb.at[s], sem_x.at[s])

    def dy_copy(t):
        return pltpu.make_async_copy(dy_h.at[0, pl.ds(t * TT, TT), :], dy.at[t], sem_dy.at[t])

    def w_copies(layer):
        return [pltpu.make_async_copy(h.at[layer], v.at[layer], sem_w.at[layer, i]) for i, (h, v) in enumerate(zip((wg_h, wu_h, wd_h), full))]

    x_copy(0).start()
    for copy in w_copies(0):
        copy.start()
    x_copy(1).start()
    for t in range(nt):
        dy_copy(t).start()
    for copy in w_copies(1):
        copy.start()
    ss[...] = jnp.zeros_like(ss)

    def gu_out(t, j):
        return pltpu.make_async_copy(da.at[j], gu_h.at[j, t], sem_gu.at[j])

    def a1t_out(t):
        p = lax.rem(t, 2)
        return pltpu.make_async_copy(wgut.at[p], a1t_h.at[t], sem_at.at[p])

    def static_block(j):
        return 2 * (j % half) + j // half

    def down_part(part):
        some = range(part * half, (part + 1) * half)
        w = jnp.concatenate([fd[0, at_block(static_block(j) + s * nc), :] for j in some for s in range(2)], 0)
        return dot(hid[:, part * half * FC:(part + 1) * half * FC], w)

    def gate_up(j):
        cols = [at_block(static_block(j) + s * nc) for s in range(2)]
        gu = dot(dgu0[...], jnp.concatenate([f[0, :, c] for f in (fg, fu) for c in cols], 1))
        da[j] = gu
        g, u = gu[:, :FC], gu[:, FC:]
        hid[:, j * FC:(j + 1) * FC] = (g * sigmoid(g) * u).astype(BF16)

    def finish(t):
        y = pg[0] + down_part(1)
        h = (xb[lax.rem(t, 3)].astype(F32) + y.astype(BF16).astype(F32)).astype(BF16)
        h1[t] = h
        wide = h.astype(F32)
        a2 = (wide * rms(wide)).astype(BF16)
        a[t] = a2
        at[t] = a2.T
        dyt[t] = dy[t].T

    def forward(t, follows):
        x_copy(t).wait()
        dy_copy(t).wait()
        if follows:
            for j in range(half):
                gu_out(t - 1, j).wait()

            @pl.when(t >= 2)
            def _():
                a1t_out(t - 2).wait()

            pg[0] = down_part(0)
        wide = xb[lax.rem(t, 3)].astype(F32)
        a1 = (wide * rms(wide)).astype(BF16)
        dgu0[...] = a1
        wgut[lax.rem(t, 2)] = a1.T
        for j in range(half):
            gate_up(j)
        for j in range(half):
            gu_out(t, j).start()
        a1t_out(t).start()
        if follows:
            for j in range(half, nc):
                gu_out(t - 1, j).wait()
            finish(t - 1)
        for j in range(half, nc):
            gate_up(j)
        for j in range(half, nc):
            gu_out(t, j).start()

        @pl.when(t + 2 < nt)
        def _():
            x_copy(t + 2).start()

    for copy in w_copies(0):
        copy.wait()
    forward(0, False)

    @pl.loop(1, nt)
    def _(t):
        forward(t, True)

    pg[0] = down_part(0)
    finish(nt - 1)
    for j in range(nc):
        gu_out(nt - 1, j).wait()
    for t in (nt - 2, nt - 1):
        a1t_out(t).wait()
    for copy in w_copies(1):
        copy.wait()

    def g_copy(u, s, way, both):
        part = (lambda ref: ref) if both else (lambda ref: ref.at[way])
        return pltpu.make_async_remote_copy(
            part(sg.at[way, s]), part(rg.at[way, lax.rem(u, 2), s]), sg_sem.at[way, s], rg_sem.at[way, lax.rem(u, 2), s],
            device_id={"dp": towards[way]}, device_id_type=MESH)

    def d_copy(j, way, both):
        k = lax.rem(j, far)
        part = (lambda ref: ref) if both else (lambda ref: ref.at[way])
        return pltpu.make_async_remote_copy(
            part(sd.at[way, k]), part(rd.at[way, k]), sd_sem.at[way, k], rd_sem.at[way, k],
            device_id={"dp": towards[way]}, device_id_type=MESH)

    def relay(u, s):
        j, slot, old = lax.rem(u, nc), lax.rem(u, UNITS_HELD), lax.rem(u, 2)
        for way in range(2):
            e = around[far - s] if way == 0 else around[n - far + s]

            @pl.when(u > 0)
            def _():
                g_copy(u - 1, s, way, s > 0).wait_send()

            if s > 0:
                g_copy(u, s - 1, way, s > 1).wait_recv()
            for h in range(2):
                if s == 0 and h != way:
                    continue
                own = pg[slot, pl.ds(pl.multiple_of(e * rows, rows), rows), h * FC:(h + 1) * FC]
                if s > 1 or (s == 1 and h == way):
                    own += rg[way, old, s - 1, h].astype(F32)
                sg[way, s, h] = own.astype(BF16)
            g_copy(u, s, way, s > 0).start()

            @pl.when(lax.rem(e, far) == lax.rem(j, far))
            def _():
                k = lax.rem(j, far)

                @pl.when(u >= far)
                def _():
                    d_copy(j, way, s > 0).wait_send()

                if s > 0:
                    d_copy(j, way, s > 1).wait_recv()
                tall = pd.shape[2] // 2
                for h in range(2):
                    if s == 0 and h != way:
                        continue
                    own = pd[slot, e // far, h * tall:(h + 1) * tall, :]
                    if s > 1 or (s == 1 and h == way):
                        own += rd[way, k, h].astype(F32)
                    sd[way, k, h] = own.astype(BF16)
                d_copy(j, way, s > 0).start()

    def square(g):
        wide = g.astype(F32)
        ss[...] += jnp.sum((wide * wide).reshape(-1, *ss.shape), 0)

    def arrive(u):
        j, slot, old, layer = lax.rem(u, nc), lax.rem(u, UNITS_HELD), lax.rem(u, 2), 1 - u // nc
        k = lax.rem(j, far)
        for way in range(2):
            g_copy(u, far - 1, way, True).wait_recv()
        for h, out in enumerate((og, ou)):
            own = pg[slot, pl.ds(pl.multiple_of(me * rows, rows), rows), h * FC:(h + 1) * FC]
            own = (own + rg[0, old, far - 1, h].astype(F32) + rg[1, old, far - 1, h].astype(F32)).astype(BF16)
            for s in range(2):
                piece = own[:, s * LB:(s + 1) * LB]
                out[layer, :, at_block(block(j) + s * nc)] = piece
                square(piece)

        @pl.when(lax.rem(me, far) == k)
        def _():
            tall = pd.shape[2] // 2
            for way in range(2):
                d_copy(j, way, True).wait_recv()
            for h in range(2):
                own = pd[slot, me // far, h * tall:(h + 1) * tall, :]
                own = own + rd[0, k, h].astype(F32) + rd[1, k, h].astype(F32)
                own = own.T.astype(BF16)
                od[layer, at_block(j // half), h * tall:(h + 1) * tall] = own
                for s in range(tall // LB):
                    square(own[:, s * LB:(s + 1) * LB])

    def turn_round(at_step):
        p, q = at_step // far, lax.rem(at_step, far)

        @pl.when((q == 0) & (p >= 4) & (p < units + 4))
        def _():
            arrive(p - 4)

        for when, s, lag in ((0, 0, 1), (1, 3, 3), (2, 2, 2), (3, 1, 1)):
            @pl.when((q == when) & (p >= lag) & (p < units + lag))
            def _(s=s, lag=lag):
                relay(p - lag, s)

    def elementwise(gu, dh, slot):
        g, u = gu[:, :FC], gu[:, FC:]
        sig = sigmoid(g)
        silu = g * sig
        hds[slot][...] = (silu * u).astype(BF16)
        dgus[slot][:, :FC] = (dh * u * (sig + silu * (1 - sig))).astype(BF16)
        dgus[slot][:, FC:] = (dh * silu).astype(BF16)

    def back(u, t, slot, first=None):
        k = lax.rem(u, UNITS_HELD)
        keep = (lambda old: old) if first is None else (lambda old: jnp.where(first, jnp.zeros_like(old), old))
        pg[k] = keep(pg[k]) + dot(at[t], dgus[slot][...])
        hd = dot(dyt[t], hds[slot][...])
        for s in range(2):
            pd[k, s] = keep(pd[k, s]) + hd[:, s * LB:(s + 1) * LB]

    def to_states(u, t, slot):
        old = jnp.where(u == 0, jnp.zeros(da.shape[1:], F32), da[t])
        da[t] = old + dot(dgus[slot][...], wgut[lax.rem(u, 2)])

    def turn(layer, j, t):
        p = lax.rem(j, 2)
        if layer:
            for i, f in enumerate((fg, fu)):
                s = lax.rem(t, 2)
                wgut[p, pl.ds(pl.multiple_of(i * FC + s * LB, LB), LB), :] = f[layer, :, at_block(block(j) + s * nc)].T
        s = lax.rem(t, 2)
        wdt[p, :, at_block(s)] = fd[layer, at_block(block(j) + s * nc), :].T

    def clear():
        for h, g in zip(hds, dgus):
            h[...] = jnp.zeros_like(h)
            g[...] = jnp.zeros_like(g)

    per_chunk = nt // 2
    pl.semaphore_wait(barrier, n - 1)

    for t in range(2):
        turn(1, 0, t)
    clear()

    def front2(j, t, slot):
        cols = [at_block(block(j) + s * nc) for s in range(2)]
        gu = dot(a[t], jnp.concatenate([f[1, :, c] for f in (fg, fu) for c in cols], 1))
        elementwise(gu, dot(dy[t], wdt[lax.rem(j, 2)]).astype(BF16).astype(F32), slot)

    @pl.loop(0, nc * per_chunk)
    def _(i):
        j, t = i // per_chunk, 2 * lax.rem(i, per_chunk)
        k = jnp.maximum(2 * i - 1, 0)
        front2(j, t, 0)
        back(k // nt, lax.rem(k, nt), 1)
        to_states(k // nt, lax.rem(k, nt), 1)
        for s in range(2):
            turn(1, jnp.minimum(j + 1, nc - 1), t + s)
        front2(j, t + 1, 1)
        back(j, t, 0, t == 0)
        to_states(j, t, 0)
        turn_round(i)

    back(nc - 1, nt - 1, 1)
    to_states(nc - 1, nt - 1, 1)

    def a1t_in(t):
        return pltpu.make_async_copy(a1t_h.at[t], at.at[t], sem_dy.at[t])

    def gu_in(i):
        return pltpu.make_async_copy(gu_h.at[i // nt, lax.rem(i, nt)], da.at[lax.rem(i, nt)], sem_gu.at[lax.rem(i, nt)])

    for t in range(nt):
        a1t_in(t).start()

    @pl.loop(0, nt)
    def _(t):
        wide = h1[t].astype(F32)
        r = rms(wide)
        da_t = da[t].astype(BF16).astype(F32)
        dn = da_t * r - wide * (r * r * r * jnp.mean(da_t * wide, -1, keepdims=True))
        dh1 = (dy[t].astype(F32) + dn).astype(BF16)
        dy[t] = dh1
        dyt[t] = dh1.T
        gu_in(t).start()
        a1t_in(t).wait()

    for t in range(2):
        turn(0, 0, t)
    clear()

    def front1(j, t, slot):
        elementwise(da[t], dot(dy[t], wdt[lax.rem(j, 2)]).astype(BF16).astype(F32), slot)

    @pl.loop(0, nc * per_chunk)
    def _(i):
        j, t = i // per_chunk, 2 * lax.rem(i, per_chunk)
        k = jnp.maximum(2 * i - 1, 0)
        for s in range(2):
            gu_in(2 * i + s).wait()
        front1(j, t, 0)
        back(nc + k // nt, lax.rem(k, nt), 1)
        for s in range(2):
            turn(0, jnp.minimum(j + 1, nc - 1), t + s)
        front1(j, t + 1, 1)
        back(nc + j, t, 0, t == 0)

        @pl.when(j + 1 < nc)
        def _():
            for s in range(2):
                gu_in(2 * i + s + nt).start()

        turn_round(nc * per_chunk + i)

    back(2 * nc - 1, nt - 1, 1)

    pieces = [(i, layer) for layer in (1, 0) for i in range(3)]
    d = h1.shape[2]
    deep = n // 2 * rows

    def moment_copies(k):
        i, layer = pieces[k]
        made = []
        for c, h in enumerate(((mg_h, mu_h, md_h)[i], (vg_h, vu_h, vd_h)[i])):
            if i == 2:
                made.append(pltpu.make_async_copy(h.at[layer], da.at[k, pl.ds(c * deep, deep), :], mv_sem.at[k, c]))
            else:
                for b in range(far):
                    made.append(pltpu.make_async_copy(
                        h.at[layer, :, pl.ds(b * d, d)], da.at[k, pl.ds(c * deep + b * rows, rows), :], mv_sem.at[k, c * far + b]))
        return made

    for k in range(len(pieces)):
        for copy in moment_copies(k):
            copy.start()

    @pl.loop(units * far, (units + 3) * far + 1)
    def _(at_step):
        turn_round(at_step)

    tots[pl.ds(me, 1)] = ss[...][None]
    totals = [
        pltpu.make_async_remote_copy(ss, tots.at[me], ts_sem.at[k], tr_sem.at[n - k], device_id={"dp": around[k]}, device_id_type=MESH)
        for k in range(1, n)
    ]
    for copy in totals:
        copy.start()
    for way in range(2):
        for s in range(far):
            g_copy(units - 1, s, way, s > 0).wait_send()
            e = around[far - s] if way == 0 else around[n - far + s]
            d_copy(lax.rem(e, far), way, s > 0).wait_send()
    for k in range(len(pieces)):
        for copy in moment_copies(k):
            copy.wait()
    for k in range(1, n):
        pltpu.make_async_remote_copy(ss, tots.at[around[k]], ts_sem.at[k], tr_sem.at[k], device_id={"dp": around[k]}, device_id_type=MESH).wait_recv()
    factor = jnp.minimum(1.0, 0.5 * lax.rsqrt(jnp.sum(tots[...], keepdims=True).reshape(1, 1) / count + 1e-30))

    def rows_of(i, origin, part=None):
        tall = full[i].shape[1] // n
        start = origin * tall
        if part is not None:
            tall //= 2
            start += part * tall
        return pl.ds(pl.multiple_of(start, tall), tall)

    def pass_on(k, s, way, coming=False):
        i, layer = pieces[k]
        back_by = s + coming
        origin = around[(n - back_by) % n] if way == 0 else around[back_by]
        here = full[i].at[layer, rows_of(i, origin, way if s == far - 1 else None), :]
        return pltpu.make_async_remote_copy(
            here, here, ag_send.at[way, s, k], ag_recv.at[way, s, k], device_id={"dp": towards[way]}, device_id_type=MESH)

    for k, (i, layer) in enumerate(pieces):
        def adamw(here, where_g, where_w):
            m_at, v_at = here, pl.ds(here.start + deep, here.size)
            g = own_g[i][(layer, *where_g)].astype(F32) * factor
            m = 0.9 * da[k, m_at, :] + 0.1 * g
            v = 0.95 * da[k, v_at, :] + 0.05 * g * g
            w = full[i][(layer, *where_w)].astype(F32)
            step = m * lax.rsqrt(v + 1e-8) + 0.1 * w
            da[k, m_at, :] = m
            da[k, v_at, :] = v
            full[i][(layer, *where_w)] = (w - 0.02 * step).astype(BF16)

        for b in range(far):
            here = pl.ds(b * rows, rows)
            if i == 2:
                adamw(here, (here, slice(None)), (pl.ds(pl.multiple_of(me * deep + b * rows, rows), rows), slice(None)))
            else:
                cols = pl.ds(b * d, d)
                adamw(here, (slice(None), cols), (pl.ds(pl.multiple_of(me * rows, rows), rows), cols))
        for way in range(2):
            pass_on(k, 0, way).start()

    for s in range(far):
        for k in range(len(pieces)):
            for way in range(2):
                pass_on(k, s, way, True).wait_recv()
                if s + 1 < far:
                    pass_on(k, s + 1, way).start()
    for copy in totals:
        copy.wait_send()
    for s in range(far):
        for k in range(len(pieces)):
            for way in range(2):
                pass_on(k, s, way).wait_send()


def flush_kernel(n, fg, fu, fd, wide, *refs):
    outs, sem = refs[:9], refs[9]
    layers, d = fg.shape[0], fg.shape[1]
    rows, far = d // n, n // 2
    deep = far * rows
    copies = []
    for k, (i, layer) in enumerate((i, layer) for layer in (1, 0) for i in range(3)):
        for c in range(2):
            out = outs[3 + 3 * c + i]
            if i == 2:
                copies.append((wide.at[k, pl.ds(c * deep, deep), :], out.at[layer]))
            else:
                copies += [(wide.at[k, pl.ds(c * deep + b * rows, rows), :], out.at[layer, :, pl.ds(b * d, d)]) for b in range(far)]
    copies += [(f.at[layer], out.at[layer]) for layer in range(layers) for f, out in zip((fg, fu, fd), outs)]
    copies = [pltpu.make_async_copy(*pair, sem.at[i]) for i, pair in enumerate(copies)]
    for copy in copies:
        copy.start()
    for copy in copies:
        copy.wait()


def train_step(x, dy, w, m, v, n):
    wg, wu, wd = w
    tokens, d = x.shape[1:]
    layers, _, f = wg.shape
    nt, nc = tokens // TT, f // FC
    far, rows = n // 2, d // n
    pieces = 3 * layers
    hbm = pl.BlockSpec(memory_space=pl.ANY)
    vmem = pl.BlockSpec(memory_space=pltpu.VMEM)
    shape = jax.ShapeDtypeStruct
    kept = [pltpu.VMEM(one.shape, BF16) for one in w] + [pltpu.VMEM((nt, TT, d), F32)]
    v_, dma = pltpu.VMEM, pltpu.SemaphoreType.DMA
    scratch = [
        v_((2, 2 * FC, d), BF16), v_((2, d, FC), BF16),
        v_((nt, TT, d), BF16), v_((nt, d, TT), BF16), v_((nt, TT, d), BF16), v_((nt, TT, d), BF16), v_((nt, d, TT), BF16),
        v_((3, TT, d), BF16), v_((TT, f), BF16), v_((TT, FC), BF16), v_((TT, FC), BF16), v_((TT, 2 * FC), BF16), v_((TT, 2 * FC), BF16),
        v_((UNITS_HELD, d, 2 * FC), F32), v_((UNITS_HELD, 2, d, LB), F32),
        v_((2, 2, far, 2, rows, FC), BF16), v_((2, far, 2, d // 2, LB), BF16), v_((2, far, 2, rows, FC), BF16), v_((2, far, 2, d // 2, LB), BF16),
        v_((layers, rows, f), BF16), v_((layers, rows, f), BF16), v_((layers, f // n, d), BF16), v_((8, LB), F32), v_((n, 8, LB), F32),
        dma((layers, 3)), dma((3,)), dma((nt,)), dma((2,)), dma((nt,)),
        dma((2, 2, far)), dma((2, far)), dma((2, far)), dma((2, far)), dma((n,)), dma((n,)),
        dma((pieces, n)), dma((2, far, pieces)), dma((2, far, pieces)),
    ]
    kept_bytes = 2 * sum(one.size for one in w) + 4 * tokens * d
    *new, wide, _, _ = pl.pallas_call(
        functools.partial(step_kernel, nt, nc, n, sum(one.size for one in w)),
        name="train_step",
        out_shape=kept + [shape((nc, nt, TT, 2 * FC), F32), shape((nt, d, TT), BF16)],
        in_specs=[hbm] * 11,
        out_specs=[vmem] * 4 + [hbm] * 2,
        scratch_shapes=scratch,
        compiler_params=pltpu.CompilerParams(vmem_limit_bytes=VMEM_BYTES - kept_bytes, collective_id=0, has_side_effects=True),
    )(x, dy, *w, *m, *v)
    copies = layers * (2 * (2 * far + 1) + 3)
    keep = lambda one: pltpu.with_memory_space_constraint(one, pltpu.VMEM)
    return tuple(pl.pallas_call(
        functools.partial(flush_kernel, n),
        name="flush",
        out_shape=[shape(one.shape, one.dtype) for group in (w, m, v) for one in group],
        in_specs=[vmem] * 4,
        out_specs=[hbm] * 9,
        scratch_shapes=[dma((copies,))],
        compiler_params=pltpu.CompilerParams(vmem_limit_bytes=1 << 20),
    )(*(keep(one) for one in (*new, wide))))


def solution(mesh):
    n = mesh.shape["dp"]

    def step(x, dy, *arrays):
        return train_step(x, dy, *(arrays[i:i + 3] for i in (0, 3, 6)), n)

    seq, rows = P(("rep", "dp"), None, None), P(None, "dp", None)
    return jax.shard_map(
        step,
        mesh=mesh,
        in_specs=(seq, seq) + (P(),) * 3 + (rows,) * 6,
        out_specs=(P("rep"),) * 3 + (P("rep", "dp"),) * 6,
        check_vma=False,
    )
```

time: 427 us -> 365 us (0.85)
  waiting for transfers between devices: 148 us -> 0 us
  Pallas kernels: 242 us -> 364 us
  between operations: 14.5 us -> 0.83 us
  other arithmetic: 11.6 us -> 0 us
  local copies, waits for them, and re-layouts: 10.7 us -> 0 us
    all_gather x3 -> x0, waiting for transfers between devices: 147 us -> none  [step(): new.append((lax.all_gather(wn, 'dp', axis=1, tiled=True), mn, vn))]
    pallas_call x1 -> x2, Pallas kernels: 242 us -> 364 us  [the longest x1 358 us: train_step(): pl.pallas_call(functools.partial(step_kernel, nt, nc, n, sum((one.size fo...]
    unnamed x13 -> x0, local copies, waits for them, and re-layouts: 10.7 us -> none
    convert_element_type x3 -> x0, other arithmetic: 10.1 us -> none  [adamw(): return ((w - 0.02 * step).astype(BF16), m, v)]
  transfers between devices with their start and end apart: 3 -> 0, of which waited for: 3 -> 0; matrix products, arithmetic and copies ran while one was open for 2% -> 0% of each run, Pallas kernels for 0% -> 0%
where the time goes in v4:
time: 365 us
  Pallas kernels  364 us (100%)
    pallas_call x1, Pallas kernels, train_step(): pl.pallas_call(functools.partial(step_kernel, nt, nc, n, sum((one.size fo...  358 us

profile of v4, /device:TPU:22, one launch (start us, length us, event | category | flops | bytes accessed | tf_op | source)
XLA Modules:
  0.0 365.3 jit_solution(16908898860907397730)
XLA Ops:
  0.6 357.6 %train_step.1 = (bf16[2,512,2048]{2,1,0:T(8,128)(2,1)S(1)}, bf16[2,512,2048]{2,1,0:T(8,128)(2,1)S(1)}, bf16[2,2048,512]{2,1,0:T(8,128)(2,1)S(1)}, f32[8,512,512]...) custom-call(bf16[1,4096,512]{2,1,0:T(8,128)(2,1)} %x_h.1, bf16[1,4096,512]{2,1,0:T(8,128)(2,1)} %dy_h.1, ...), custom_call_target="tpu_custom_call" | custom-call | tf_op jit(solution)/shard_map/train_step/pallas_call | solution.py:507
  358.3 6.8 %flush.1 = (bf16[2,512,2048]{2,1,0:T(8,128)(2,1)}, bf16[2,512,2048]{2,1,0:T(8,128)(2,1)}, bf16[2,2048,512]{2,1,0:T(8,128)(2,1)}, f32[2,64,2048]{2,1,0:T(8,128)},...) custom-call(bf16[2,512,2048]{2,1,0:T(8,128)(2,1)S(1)} %get-tuple-ele, ...), custom_call_target="tpu_custom_call" | custom-call | tf_op jit(solution)/shard_map/flush/pallas_call | solution.py:518

commit v5 on v4

--- a/solution.py
+++ b/solution.py
@@ -12,7 +12,7 @@
 TT = 512
 LB = 128
 FC = 2 * LB
-UNITS_HELD = 5
+UNITS_HELD = 7
 VMEM_BYTES = 67_043_328
 
 
@@ -30,8 +30,8 @@
 
 def step_kernel(nt, nc, n, count, x_h, dy_h, wg_h, wu_h, wd_h, mg_h, mu_h, md_h, vg_h, vu_h, vd_h,
                 fg, fu, fd, wide_ref, gu_h, a1t_h,
-                wgut, wdt, a, at, h1, dy, dyt, xb, hid, hd0, hd1, dgu0, dgu1,
-                pg, pd, rg, rd, sg, sd, og, ou, od, ss, tots,
+                wgut, wdt, a, at, h1, dy, dyt, hid, hd0, hd1, dgu0, dgu1,
+                pg, pd, rg, sg, og, ou, od, ss, tots,
                 sem_w, sem_x, sem_dy, sem_at, sem_gu, rg_sem, rd_sem, sg_sem, sd_sem, ts_sem, tr_sem, mv_sem, ag_send, ag_recv):
     half, far = nc // 2, n // 2
     units = 2 * nc
@@ -43,10 +43,6 @@
     around = [lax.rem(me + k, n) for k in range(n)]
     towards = (around[1], around[n - 1])
 
-    barrier = pltpu.get_barrier_semaphore()
-    for k in range(1, n):
-        pl.semaphore_signal(barrier, inc=1, device_id={"dp": around[k]}, device_id_type=MESH)
-
     def block(j):
         return 2 * lax.rem(j, half) + j // half
 
@@ -54,8 +50,7 @@
         return pl.ds(b * LB if isinstance(b, int) else pl.multiple_of(b * LB, LB), LB)
 
     def x_copy(t):
-        s = lax.rem(t, 3)
-        return pltpu.make_async_copy(x_h.at[0, pl.ds(t * TT, TT), :], xb.at[s], sem_x.at[s])
+        return pltpu.make_async_copy(x_h.at[0, pl.ds(t * TT, TT), :], a.at[t], sem_x.at[t])
 
     def dy_copy(t):
         return pltpu.make_async_copy(dy_h.at[0, pl.ds(t * TT, TT), :], dy.at[t], sem_dy.at[t])
@@ -66,8 +61,9 @@
     x_copy(0).start()
     for copy in w_copies(0):
         copy.start()
-    x_copy(1).start()
     for t in range(nt):
+        if t:
+            x_copy(t).start()
         dy_copy(t).start()
     for copy in w_copies(1):
         copy.start()
@@ -86,18 +82,20 @@
     def down_part(part):
         some = range(part * half, (part + 1) * half)
         w = jnp.concatenate([fd[0, at_block(static_block(j) + s * nc), :] for j in some for s in range(2)], 0)
-        return dot(hid[:, part * half * FC:(part + 1) * half * FC], w)
+        return dot(jnp.concatenate([hid[b] for b in range(part * nc, (part + 1) * nc)], 1), w)
 
     def gate_up(j):
         cols = [at_block(static_block(j) + s * nc) for s in range(2)]
         gu = dot(dgu0[...], jnp.concatenate([f[0, :, c] for f in (fg, fu) for c in cols], 1))
         da[j] = gu
         g, u = gu[:, :FC], gu[:, FC:]
-        hid[:, j * FC:(j + 1) * FC] = (g * sigmoid(g) * u).astype(BF16)
+        h = (g * sigmoid(g) * u).astype(BF16)
+        for s in range(2):
+            hid[2 * j + s] = h[:, s * LB:(s + 1) * LB]
 
     def finish(t):
         y = pg[0] + down_part(1)
-        h = (xb[lax.rem(t, 3)].astype(F32) + y.astype(BF16).astype(F32)).astype(BF16)
+        h = (a[t].astype(F32) + y.astype(BF16).astype(F32)).astype(BF16)
         h1[t] = h
         wide = h.astype(F32)
         a2 = (wide * rms(wide)).astype(BF16)
@@ -117,7 +115,7 @@
                 a1t_out(t - 2).wait()
 
             pg[0] = down_part(0)
-        wide = xb[lax.rem(t, 3)].astype(F32)
+        wide = a[t].astype(F32)
         a1 = (wide * rms(wide)).astype(BF16)
         dgu0[...] = a1
         wgut[lax.rem(t, 2)] = a1.T
@@ -135,10 +133,6 @@
         for j in range(half, nc):
             gu_out(t, j).start()
 
-        @pl.when(t + 2 < nt)
-        def _():
-            x_copy(t + 2).start()
-
     for copy in w_copies(0):
         copy.wait()
     forward(0, False)
@@ -156,27 +150,37 @@
     for copy in w_copies(1):
         copy.wait()
 
+    barrier = pltpu.get_barrier_semaphore()
+    for k in range(1, n):
+        pl.semaphore_signal(barrier, inc=1, device_id={"dp": around[k]}, device_id_type=MESH)
+
     def g_copy(u, s, way, both):
         part = (lambda ref: ref) if both else (lambda ref: ref.at[way])
+        old, new = lax.rem(u, 2), lax.rem(u, 4)
         return pltpu.make_async_remote_copy(
-            part(sg.at[way, s]), part(rg.at[way, lax.rem(u, 2), s]), sg_sem.at[way, s], rg_sem.at[way, lax.rem(u, 2), s],
+            part(sg.at[way, old, s]), part(rg.at[way, new, s]), sg_sem.at[way, old, s], rg_sem.at[way, new, s],
             device_id={"dp": towards[way]}, device_id_type=MESH)
+
+    tall = pd.shape[2] // 2
+
+    def d_at(way, k, sent):
+        return hid.at[(2 * sent + way) * far + k]
 
     def d_copy(j, way, both):
         k = lax.rem(j, far)
-        part = (lambda ref: ref) if both else (lambda ref: ref.at[way])
+        part = (lambda ref: ref) if both else (lambda ref: ref.at[pl.ds(way * tall, tall), :])
         return pltpu.make_async_remote_copy(
-            part(sd.at[way, k]), part(rd.at[way, k]), sd_sem.at[way, k], rd_sem.at[way, k],
+            part(d_at(way, k, 1)), part(d_at(way, k, 0)), sd_sem.at[way, k], rd_sem.at[way, k],
             device_id={"dp": towards[way]}, device_id_type=MESH)
 
     def relay(u, s):
-        j, slot, old = lax.rem(u, nc), lax.rem(u, UNITS_HELD), lax.rem(u, 2)
+        j, slot, old, new = lax.rem(u, nc), lax.rem(u, UNITS_HELD), lax.rem(u, 2), lax.rem(u, 4)
         for way in range(2):
             e = around[far - s] if way == 0 else around[n - far + s]
 
-            @pl.when(u > 0)
+            @pl.when(u > 1)
             def _():
-                g_copy(u - 1, s, way, s > 0).wait_send()
+                g_copy(u - 2, s, way, s > 0).wait_send()
 
             if s > 0:
                 g_copy(u, s - 1, way, s > 1).wait_recv()
@@ -185,8 +189,8 @@
                     continue
                 own = pg[slot, pl.ds(pl.multiple_of(e * rows, rows), rows), h * FC:(h + 1) * FC]
                 if s > 1 or (s == 1 and h == way):
-                    own += rg[way, old, s - 1, h].astype(F32)
-                sg[way, s, h] = own.astype(BF16)
+                    own += rg[way, new, s - 1, h].astype(F32)
+                sg[way, old, s, h] = own.astype(BF16)
             g_copy(u, s, way, s > 0).start()
 
             @pl.when(lax.rem(e, far) == lax.rem(j, far))
@@ -199,14 +203,14 @@
 
                 if s > 0:
                     d_copy(j, way, s > 1).wait_recv()
-                tall = pd.shape[2] // 2
                 for h in range(2):
                     if s == 0 and h != way:
                         continue
-                    own = pd[slot, e // far, h * tall:(h + 1) * tall, :]
+                    part = pl.ds(h * tall, tall)
+                    own = pd[slot, e // far, part, :]
                     if s > 1 or (s == 1 and h == way):
-                        own += rd[way, k, h].astype(F32)
-                    sd[way, k, h] = own.astype(BF16)
+                        own += d_at(way, k, 0)[part, :].astype(F32)
+                    d_at(way, k, 1)[part, :] = own.astype(BF16)
                 d_copy(j, way, s > 0).start()
 
     def square(g):
@@ -214,7 +218,7 @@
         ss[...] += jnp.sum((wide * wide).reshape(-1, *ss.shape), 0)
 
     def arrive(u):
-        j, slot, old, layer = lax.rem(u, nc), lax.rem(u, UNITS_HELD), lax.rem(u, 2), 1 - u // nc
+        j, slot, old, layer = lax.rem(u, nc), lax.rem(u, UNITS_HELD), lax.rem(u, 4), 1 - u // nc
         k = lax.rem(j, far)
         for way in range(2):
             g_copy(u, far - 1, way, True).wait_recv()
@@ -228,12 +232,12 @@
 
         @pl.when(lax.rem(me, far) == k)
         def _():
-            tall = pd.shape[2] // 2
             for way in range(2):
                 d_copy(j, way, True).wait_recv()
             for h in range(2):
-                own = pd[slot, me // far, h * tall:(h + 1) * tall, :]
-                own = own + rd[0, k, h].astype(F32) + rd[1, k, h].astype(F32)
+                part = pl.ds(h * tall, tall)
+                own = pd[slot, me // far, part, :]
+                own = own + d_at(0, k, 0)[part, :].astype(F32) + d_at(1, k, 0)[part, :].astype(F32)
                 own = own.T.astype(BF16)
                 od[layer, at_block(j // half), h * tall:(h + 1) * tall] = own
                 for s in range(tall // LB):
@@ -242,11 +246,11 @@
     def turn_round(at_step):
         p, q = at_step // far, lax.rem(at_step, far)
 
-        @pl.when((q == 0) & (p >= 4) & (p < units + 4))
+        @pl.when((q == 0) & (p >= 6) & (p < units + 6))
         def _():
-            arrive(p - 4)
-
-        for when, s, lag in ((0, 0, 1), (1, 3, 3), (2, 2, 2), (3, 1, 1)):
+            arrive(p - 6)
+
+        for when, s, lag in ((0, 0, 1), (1, 1, 2), (2, 2, 3), (3, 3, 4)):
             @pl.when((q == when) & (p >= lag) & (p < units + lag))
             def _(s=s, lag=lag):
                 relay(p - lag, s)
@@ -384,7 +388,7 @@
         for copy in moment_copies(k):
             copy.start()
 
-    @pl.loop(units * far, (units + 3) * far + 1)
+    @pl.loop(units * far, (units + 5) * far + 1)
     def _(at_step):
         turn_round(at_step)
 
@@ -397,7 +401,8 @@
         copy.start()
     for way in range(2):
         for s in range(far):
-            g_copy(units - 1, s, way, s > 0).wait_send()
+            for u in (units - 2, units - 1):
+                g_copy(u, s, way, s > 0).wait_send()
             e = around[far - s] if way == 0 else around[n - far + s]
             d_copy(lax.rem(e, far), way, s > 0).wait_send()
     for k in range(len(pieces)):
@@ -495,12 +500,12 @@
     scratch = [
         v_((2, 2 * FC, d), BF16), v_((2, d, FC), BF16),
         v_((nt, TT, d), BF16), v_((nt, d, TT), BF16), v_((nt, TT, d), BF16), v_((nt, TT, d), BF16), v_((nt, d, TT), BF16),
-        v_((3, TT, d), BF16), v_((TT, f), BF16), v_((TT, FC), BF16), v_((TT, FC), BF16), v_((TT, 2 * FC), BF16), v_((TT, 2 * FC), BF16),
+        v_((2 * nc, TT, LB), BF16), v_((TT, FC), BF16), v_((TT, FC), BF16), v_((TT, 2 * FC), BF16), v_((TT, 2 * FC), BF16),
         v_((UNITS_HELD, d, 2 * FC), F32), v_((UNITS_HELD, 2, d, LB), F32),
-        v_((2, 2, far, 2, rows, FC), BF16), v_((2, far, 2, d // 2, LB), BF16), v_((2, far, 2, rows, FC), BF16), v_((2, far, 2, d // 2, LB), BF16),
+        v_((2, 4, far, 2, rows, FC), BF16), v_((2, 2, far, 2, rows, FC), BF16),
         v_((layers, rows, f), BF16), v_((layers, rows, f), BF16), v_((layers, f // n, d), BF16), v_((8, LB), F32), v_((n, 8, LB), F32),
-        dma((layers, 3)), dma((3,)), dma((nt,)), dma((2,)), dma((nt,)),
-        dma((2, 2, far)), dma((2, far)), dma((2, far)), dma((2, far)), dma((n,)), dma((n,)),
+        dma((layers, 3)), dma((nt,)), dma((nt,)), dma((2,)), dma((nt,)),
+        dma((2, 4, far)), dma((2, far)), dma((2, 2, far)), dma((2, far)), dma((n,)), dma((n,)),
         dma((pieces, n)), dma((2, far, pieces)), dma((2, far, pieces)),
     ]
     kept_bytes = 2 * sum(one.size for one in w) + 4 * tokens * d

time: 365 us -> 362 us (level)
  no operation moved by 1% of the time
where the time goes in v5:
time: 362 us
  Pallas kernels  361 us (100%)
    pallas_call x1, Pallas kernels, train_step(): pl.pallas_call(functools.partial(step_kernel, nt, nc, n, sum((one.size fo...  355 us

profile of v5, /device:TPU:22, one launch (start us, length us, event | category | flops | bytes accessed | tf_op | source)
XLA Modules:
  0.0 362.2 jit_solution(15159770365319406761)
XLA Ops:
  0.6 354.5 %train_step.1 = (bf16[2,512,2048]{2,1,0:T(8,128)(2,1)S(1)}, bf16[2,512,2048]{2,1,0:T(8,128)(2,1)S(1)}, bf16[2,2048,512]{2,1,0:T(8,128)(2,1)S(1)}, f32[8,512,512]...) custom-call(bf16[1,4096,512]{2,1,0:T(8,128)(2,1)} %x_h.1, bf16[1,4096,512]{2,1,0:T(8,128)(2,1)} %dy_h.1, ...), custom_call_target="tpu_custom_call" | custom-call | tf_op jit(solution)/shard_map/train_step/pallas_call | solution.py:512
  355.2 6.8 %flush.1 = (bf16[2,512,2048]{2,1,0:T(8,128)(2,1)}, bf16[2,512,2048]{2,1,0:T(8,128)(2,1)}, bf16[2,2048,512]{2,1,0:T(8,128)(2,1)}, f32[2,64,2048]{2,1,0:T(8,128)},...) custom-call(bf16[2,512,2048]{2,1,0:T(8,128)(2,1)S(1)} %get-tuple-ele, ...), custom_call_target="tpu_custom_call" | custom-call | tf_op jit(solution)/shard_map/flush/pallas_call | solution.py:523

commit v6 on v5

--- a/solution.py
+++ b/solution.py
@@ -61,12 +61,6 @@
     x_copy(0).start()
     for copy in w_copies(0):
         copy.start()
-    for t in range(nt):
-        if t:
-            x_copy(t).start()
-        dy_copy(t).start()
-    for copy in w_copies(1):
-        copy.start()
     ss[...] = jnp.zeros_like(ss)
 
     def gu_out(t, j):
@@ -94,19 +88,17 @@
             hid[2 * j + s] = h[:, s * LB:(s + 1) * LB]
 
     def finish(t):
-        y = pg[0] + down_part(1)
-        h = (a[t].astype(F32) + y.astype(BF16).astype(F32)).astype(BF16)
+        h = (a[t].astype(F32) + pg[0].astype(BF16).astype(F32)).astype(BF16)
         h1[t] = h
         wide = h.astype(F32)
         a2 = (wide * rms(wide)).astype(BF16)
         a[t] = a2
         at[t] = a2.T
-        dyt[t] = dy[t].T
 
     def forward(t, follows):
         x_copy(t).wait()
-        dy_copy(t).wait()
         if follows:
+            dy_copy(t - 1).wait()
             for j in range(half):
                 gu_out(t - 1, j).wait()
 
@@ -119,6 +111,8 @@
         a1 = (wide * rms(wide)).astype(BF16)
         dgu0[...] = a1
         wgut[lax.rem(t, 2)] = a1.T
+        if follows:
+            dyt[t - 1] = dy[t - 1].T
         for j in range(half):
             gate_up(j)
         for j in range(half):
@@ -127,21 +121,31 @@
         if follows:
             for j in range(half, nc):
                 gu_out(t - 1, j).wait()
+            pg[0] += down_part(1)
+        for j in range(half, nc):
+            gate_up(j)
+        if follows:
             finish(t - 1)
         for j in range(half, nc):
-            gate_up(j)
-        for j in range(half, nc):
             gu_out(t, j).start()
 
     for copy in w_copies(0):
         copy.wait()
+    dy_copy(0).start()
+    for t in range(1, nt):
+        x_copy(t).start()
+        dy_copy(t).start()
+    for copy in w_copies(1):
+        copy.start()
     forward(0, False)
 
     @pl.loop(1, nt)
     def _(t):
         forward(t, True)
 
-    pg[0] = down_part(0)
+    pg[0] = down_part(0) + down_part(1)
+    dy_copy(nt - 1).wait()
+    dyt[nt - 1] = dy[nt - 1].T
     finish(nt - 1)
     for j in range(nc):
         gu_out(nt - 1, j).wait()
@@ -263,10 +267,15 @@
         dgus[slot][:, :FC] = (dh * u * (sig + silu * (1 - sig))).astype(BF16)
         dgus[slot][:, FC:] = (dh * silu).astype(BF16)
 
-    def back(u, t, slot, first=None):
-        k = lax.rem(u, UNITS_HELD)
-        keep = (lambda old: old) if first is None else (lambda old: jnp.where(first, jnp.zeros_like(old), old))
+    def keep_from(first):
+        return (lambda old: old) if first is None else (lambda old: jnp.where(first, jnp.zeros_like(old), old))
+
+    def back_g(u, t, slot, first=None):
+        k, keep = lax.rem(u, UNITS_HELD), keep_from(first)
         pg[k] = keep(pg[k]) + dot(at[t], dgus[slot][...])
+
+    def back_d(u, t, slot, first=None):
+        k, keep = lax.rem(u, UNITS_HELD), keep_from(first)
         hd = dot(dyt[t], hds[slot][...])
         for s in range(2):
             pd[k, s] = keep(pd[k, s]) + hd[:, s * LB:(s + 1) * LB]
@@ -305,18 +314,22 @@
     def _(i):
         j, t = i // per_chunk, 2 * lax.rem(i, per_chunk)
         k = jnp.maximum(2 * i - 1, 0)
+        jk, tk, jn = k // nt, lax.rem(k, nt), jnp.minimum(j + 1, nc - 1)
+        to_states(jk, tk, 1)
+        back_d(jk, tk, 1)
         front2(j, t, 0)
-        back(k // nt, lax.rem(k, nt), 1)
-        to_states(k // nt, lax.rem(k, nt), 1)
-        for s in range(2):
-            turn(1, jnp.minimum(j + 1, nc - 1), t + s)
+        to_states(j, t, 0)
+        back_g(jk, tk, 1)
+        turn(1, jn, t + 1)
+        back_d(j, t, 0, t == 0)
+        turn(1, jn, t)
         front2(j, t + 1, 1)
-        back(j, t, 0, t == 0)
-        to_states(j, t, 0)
+        back_g(j, t, 0, t == 0)
         turn_round(i)
 
-    back(nc - 1, nt - 1, 1)
     to_states(nc - 1, nt - 1, 1)
+    back_d(nc - 1, nt - 1, 1)
+    back_g(nc - 1, nt - 1, 1)
 
     def a1t_in(t):
         return pltpu.make_async_copy(a1t_h.at[t], at.at[t], sem_dy.at[t])
@@ -352,12 +365,15 @@
         k = jnp.maximum(2 * i - 1, 0)
         for s in range(2):
             gu_in(2 * i + s).wait()
+        jk, tk, jn = nc + k // nt, lax.rem(k, nt), jnp.minimum(j + 1, nc - 1)
+        turn(0, jn, t + 1)
+        back_d(jk, tk, 1)
+        turn(0, jn, t)
+        back_g(jk, tk, 1)
         front1(j, t, 0)
-        back(nc + k // nt, lax.rem(k, nt), 1)
-        for s in range(2):
-            turn(0, jnp.minimum(j + 1, nc - 1), t + s)
+        back_d(nc + j, t, 0, t == 0)
         front1(j, t + 1, 1)
-        back(nc + j, t, 0, t == 0)
+        back_g(nc + j, t, 0, t == 0)
 
         @pl.when(j + 1 < nc)
         def _():
@@ -366,7 +382,8 @@
 
         turn_round(nc * per_chunk + i)
 
-    back(2 * nc - 1, nt - 1, 1)
+    back_d(2 * nc - 1, nt - 1, 1)
+    back_g(2 * nc - 1, nt - 1, 1)
 
     pieces = [(i, layer) for layer in (1, 0) for i in range(3)]
     d = h1.shape[2]

time: 362 us -> 357 us (0.986)
  Pallas kernels: 361 us -> 356 us
    pallas_call x1, Pallas kernels: 355 us -> 350 us  [train_step(): pl.pallas_call(functools.partial(step_kernel, nt, nc, n, sum((one.size fo...]
where the time goes in v6:
time: 357 us
  Pallas kernels  356 us (100%)
    pallas_call x1, Pallas kernels, train_step(): pl.pallas_call(functools.partial(step_kernel, nt, nc, n, sum((one.size fo...  350 us

profile of v6, /device:TPU:22, one launch (start us, length us, event | category | flops | bytes accessed | tf_op | source)
XLA Modules:
  0.0 357.3 jit_solution(6683242956202305362)
XLA Ops:
  0.6 349.6 %train_step.1 = (bf16[2,512,2048]{2,1,0:T(8,128)(2,1)S(1)}, bf16[2,512,2048]{2,1,0:T(8,128)(2,1)S(1)}, bf16[2,2048,512]{2,1,0:T(8,128)(2,1)S(1)}, f32[8,512,512]...) custom-call(bf16[1,4096,512]{2,1,0:T(8,128)(2,1)} %x_h.1, bf16[1,4096,512]{2,1,0:T(8,128)(2,1)} %dy_h.1, ...), custom_call_target="tpu_custom_call" | custom-call | tf_op jit(solution)/shard_map/train_step/pallas_call | solution.py:529
  350.3 6.8 %flush.1 = (bf16[2,512,2048]{2,1,0:T(8,128)(2,1)}, bf16[2,512,2048]{2,1,0:T(8,128)(2,1)}, bf16[2,2048,512]{2,1,0:T(8,128)(2,1)}, f32[2,64,2048]{2,1,0:T(8,128)},...) custom-call(bf16[2,512,2048]{2,1,0:T(8,128)(2,1)S(1)} %get-tuple-ele, ...), custom_call_target="tpu_custom_call" | custom-call | tf_op jit(solution)/shard_map/flush/pallas_call | solution.py:540

commit v7 on v6

--- a/solution.py
+++ b/solution.py
@@ -32,7 +32,7 @@
                 fg, fu, fd, wide_ref, gu_h, a1t_h,
                 wgut, wdt, a, at, h1, dy, dyt, hid, hd0, hd1, dgu0, dgu1,
                 pg, pd, rg, sg, og, ou, od, ss, tots,
-                sem_w, sem_x, sem_dy, sem_at, sem_gu, rg_sem, rd_sem, sg_sem, sd_sem, ts_sem, tr_sem, mv_sem, ag_send, ag_recv):
+                sem_w, sem_x, sem_dy, sem_at, sem_gu, sem_gi, rg_sem, rd_sem, sg_sem, sd_sem, ts_sem, tr_sem, mv_sem, ag_send, ag_recv):
     half, far = nc // 2, n // 2
     units = 2 * nc
     rows = pg.shape[1] // n
@@ -63,8 +63,19 @@
         copy.start()
     ss[...] = jnp.zeros_like(ss)
 
-    def gu_out(t, j):
-        return pltpu.make_async_copy(da.at[j], gu_h.at[j, t], sem_gu.at[j])
+    def staged(odd, j):
+        if not odd:
+            return [(da.at[j], 0, 2 * FC)]
+        if j < UNITS_HELD:
+            return [(pg.at[j], 0, 2 * FC)]
+        return [(pd.at[UNITS_HELD - 2 + i // 2, i % 2], i * LB, LB) for i in range(2 * FC // LB)]
+
+    def gu_out(t, odd, j):
+        return [pltpu.make_async_copy(ref, gu_h.at[j, t, :, pl.ds(at_, width)], sem_gu.at[odd * (nc + 3) + j + i])
+                for i, (ref, at_, width) in enumerate(staged(odd, j))]
+
+    def gu_out_all(t, odd):
+        return [copy for j in range(nc) for copy in gu_out(t, odd, j)]
 
     def a1t_out(t):
         p = lax.rem(t, 2)
@@ -73,61 +84,53 @@
     def static_block(j):
         return 2 * (j % half) + j // half
 
-    def down_part(part):
-        some = range(part * half, (part + 1) * half)
-        w = jnp.concatenate([fd[0, at_block(static_block(j) + s * nc), :] for j in some for s in range(2)], 0)
-        return dot(jnp.concatenate([hid[b] for b in range(part * nc, (part + 1) * nc)], 1), w)
-
-    def gate_up(j):
+    def down():
+        w = jnp.concatenate([fd[0, at_block(static_block(j) + s * nc), :] for j in range(nc) for s in range(2)], 0)
+        return dot(jnp.concatenate([hid[b] for b in range(2 * nc)], 1), w)
+
+    def gate_up(odd, j):
         cols = [at_block(static_block(j) + s * nc) for s in range(2)]
         gu = dot(dgu0[...], jnp.concatenate([f[0, :, c] for f in (fg, fu) for c in cols], 1))
-        da[j] = gu
+        for ref, at_, width in staged(odd, j):
+            ref[...] = gu[:, at_:at_ + width]
         g, u = gu[:, :FC], gu[:, FC:]
         h = (g * sigmoid(g) * u).astype(BF16)
         for s in range(2):
             hid[2 * j + s] = h[:, s * LB:(s + 1) * LB]
 
-    def finish(t):
-        h = (a[t].astype(F32) + pg[0].astype(BF16).astype(F32)).astype(BF16)
+    def finish(t, y):
+        h = (a[t].astype(F32) + y.astype(BF16).astype(F32)).astype(BF16)
         h1[t] = h
         wide = h.astype(F32)
         a2 = (wide * rms(wide)).astype(BF16)
         a[t] = a2
         at[t] = a2.T
-
-    def forward(t, follows):
+        dyt[t] = dy[t].T
+
+    def forward(t, odd, follows):
         x_copy(t).wait()
         if follows:
             dy_copy(t - 1).wait()
-            for j in range(half):
-                gu_out(t - 1, j).wait()
-
-            @pl.when(t >= 2)
-            def _():
-                a1t_out(t - 2).wait()
-
-            pg[0] = down_part(0)
+
+        @pl.when(t >= 2)
+        def _():
+            a1t_out(t - 2).wait()
+            for copy in gu_out_all(t - 2, odd):
+                copy.wait()
+
+        if follows:
+            y = down()
         wide = a[t].astype(F32)
         a1 = (wide * rms(wide)).astype(BF16)
         dgu0[...] = a1
         wgut[lax.rem(t, 2)] = a1.T
-        if follows:
-            dyt[t - 1] = dy[t - 1].T
-        for j in range(half):
-            gate_up(j)
-        for j in range(half):
-            gu_out(t, j).start()
+        for j in range(nc):
+            gate_up(odd, j)
+            if j == half and follows:
+                finish(t - 1, y)
+        for copy in gu_out_all(t, odd):
+            copy.start()
         a1t_out(t).start()
-        if follows:
-            for j in range(half, nc):
-                gu_out(t - 1, j).wait()
-            pg[0] += down_part(1)
-        for j in range(half, nc):
-            gate_up(j)
-        if follows:
-            finish(t - 1)
-        for j in range(half, nc):
-            gu_out(t, j).start()
 
     for copy in w_copies(0):
         copy.wait()
@@ -137,20 +140,22 @@
         dy_copy(t).start()
     for copy in w_copies(1):
         copy.start()
-    forward(0, False)
-
-    @pl.loop(1, nt)
-    def _(t):
-        forward(t, True)
-
-    pg[0] = down_part(0) + down_part(1)
+    forward(0, 0, False)
+
+    @pl.loop(0, nt // 2 - 1)
+    def _(i):
+        forward(2 * i + 1, 1, True)
+        forward(2 * i + 2, 0, True)
+
+    forward(nt - 1, 1, True)
     dy_copy(nt - 1).wait()
-    dyt[nt - 1] = dy[nt - 1].T
-    finish(nt - 1)
-    for j in range(nc):
-        gu_out(nt - 1, j).wait()
+    finish(nt - 1, down())
+    for copy in gu_out_all(nt - 2, 0):
+        copy.wait()
     for t in (nt - 2, nt - 1):
         a1t_out(t).wait()
+    for copy in gu_out(nt - 1, 1, 0):
+        copy.wait()
     for copy in w_copies(1):
         copy.wait()
 
@@ -314,6 +319,11 @@
     def _(i):
         j, t = i // per_chunk, 2 * lax.rem(i, per_chunk)
         k = jnp.maximum(2 * i - 1, 0)
+        @pl.when(i == 2)
+        def _():
+            for copy in [c for k in range(1, nc) for c in gu_out(nt - 1, 1, k)]:
+                copy.wait()
+
         jk, tk, jn = k // nt, lax.rem(k, nt), jnp.minimum(j + 1, nc - 1)
         to_states(jk, tk, 1)
         back_d(jk, tk, 1)
@@ -335,7 +345,7 @@
         return pltpu.make_async_copy(a1t_h.at[t], at.at[t], sem_dy.at[t])
 
     def gu_in(i):
-        return pltpu.make_async_copy(gu_h.at[i // nt, lax.rem(i, nt)], da.at[lax.rem(i, nt)], sem_gu.at[lax.rem(i, nt)])
+        return pltpu.make_async_copy(gu_h.at[i // nt, lax.rem(i, nt)], da.at[lax.rem(i, nt)], sem_gi.at[lax.rem(i, nt)])
 
     for t in range(nt):
         a1t_in(t).start()
@@ -521,7 +531,7 @@
         v_((UNITS_HELD, d, 2 * FC), F32), v_((UNITS_HELD, 2, d, LB), F32),
         v_((2, 4, far, 2, rows, FC), BF16), v_((2, 2, far, 2, rows, FC), BF16),
         v_((layers, rows, f), BF16), v_((layers, rows, f), BF16), v_((layers, f // n, d), BF16), v_((8, LB), F32), v_((n, 8, LB), F32),
-        dma((layers, 3)), dma((nt,)), dma((nt,)), dma((2,)), dma((nt,)),
+        dma((layers, 3)), dma((nt,)), dma((nt,)), dma((2,)), dma((2 * nc + 6,)), dma((nt,)),
         dma((2, 4, far)), dma((2, far)), dma((2, 2, far)), dma((2, far)), dma((n,)), dma((n,)),
         dma((pieces, n)), dma((2, far, pieces)), dma((2, far, pieces)),
     ]

time: 357 us -> 356 us (level)
  no operation moved by 1% of the time
where the time goes in v7:
time: 356 us
  Pallas kernels  355 us (100%)
    pallas_call x1, Pallas kernels, train_step(): pl.pallas_call(functools.partial(step_kernel, nt, nc, n, sum((one.size fo...  348 us

profile of v7, /device:TPU:22, one launch (start us, length us, event | category | flops | bytes accessed | tf_op | source)
XLA Modules:
  0.0 356.0 jit_solution(4363204816767787215)
XLA Ops:
  0.6 348.3 %train_step.1 = (bf16[2,512,2048]{2,1,0:T(8,128)(2,1)S(1)}, bf16[2,512,2048]{2,1,0:T(8,128)(2,1)S(1)}, bf16[2,2048,512]{2,1,0:T(8,128)(2,1)S(1)}, f32[8,512,512]...) custom-call(bf16[1,4096,512]{2,1,0:T(8,128)(2,1)} %x_h.1, bf16[1,4096,512]{2,1,0:T(8,128)(2,1)} %dy_h.1, ...), custom_call_target="tpu_custom_call" | custom-call | tf_op jit(solution)/shard_map/train_step/pallas_call | solution.py:539
  349.0 6.8 %flush.1 = (bf16[2,512,2048]{2,1,0:T(8,128)(2,1)}, bf16[2,512,2048]{2,1,0:T(8,128)(2,1)}, bf16[2,2048,512]{2,1,0:T(8,128)(2,1)}, f32[2,64,2048]{2,1,0:T(8,128)},...) custom-call(bf16[2,512,2048]{2,1,0:T(8,128)(2,1)S(1)} %get-tuple-ele, ...), custom_call_target="tpu_custom_call" | custom-call | tf_op jit(solution)/shard_map/flush/pallas_call | solution.py:550

commit v8 on v7

--- a/solution.py
+++ b/solution.py
@@ -12,8 +12,22 @@
 TT = 512
 LB = 128
 FC = 2 * LB
+RECEIVED = 6
 UNITS_HELD = 7
 VMEM_BYTES = 67_043_328
+PLACES = (
+    (4, 8, 13, 16, 20, 25, 28, 33, 40, 44, 48, 52, 56, 61, 64),
+    (6, 11, 16, 19, 23, 28, 35, 39, 46, 48, 54, 57, 60, 66),
+    (9, 14, 18, 24, 26, 31, 41, 45, 51, 53, 59, 63, 64),
+    (12, 17, 21, 29, 30, 36, 48, 50, 56, 61, 65),
+    (18, 20, 31, 37, 41, 49, 53, 56, 63),
+)
+LAST = (
+    ("g", 9, 4), ("g", 15, 0), ("g", 11, 3), ("g", 12, 3), ("d", 15, 0), ("d", 9, 4), ("d", 11, 3), ("d", 12, 3), ("d", 14, 1),
+    ("d", 13, 2), ("g", 14, 1), ("g", 10, 4), ("d", 10, 4), ("g", 15, 1), ("g", 13, 2), ("g", 11, 4), ("g", 12, 4), ("d", 15, 1),
+    ("d", 14, 2), ("g", 14, 2), ("d", 11, 4), ("g", 15, 2), ("d", 13, 3), ("d", 12, 4), ("g", 13, 3), ("d", 15, 2), ("d", 14, 3),
+    ("g", 14, 3), ("g", 15, 3), ("d", 15, 3), ("d", 13, 4), ("g", 13, 4), ("d", 14, 4), ("g", 14, 4), ("g", 15, 4), ("d", 15, 4),
+)
 
 
 def dot(a, b):
@@ -165,7 +179,7 @@
 
     def g_copy(u, s, way, both):
         part = (lambda ref: ref) if both else (lambda ref: ref.at[way])
-        old, new = lax.rem(u, 2), lax.rem(u, 4)
+        old, new = lax.rem(u, 2), lax.rem(u, RECEIVED)
         return pltpu.make_async_remote_copy(
             part(sg.at[way, old, s]), part(rg.at[way, new, s]), sg_sem.at[way, old, s], rg_sem.at[way, new, s],
             device_id={"dp": towards[way]}, device_id_type=MESH)
@@ -182,8 +196,8 @@
             part(d_at(way, k, 1)), part(d_at(way, k, 0)), sd_sem.at[way, k], rd_sem.at[way, k],
             device_id={"dp": towards[way]}, device_id_type=MESH)
 
-    def relay(u, s):
-        j, slot, old, new = lax.rem(u, nc), lax.rem(u, UNITS_HELD), lax.rem(u, 2), lax.rem(u, 4)
+    def relay_g(u, s):
+        slot, old, new = lax.rem(u, UNITS_HELD), lax.rem(u, 2), lax.rem(u, RECEIVED)
         for way in range(2):
             e = around[far - s] if way == 0 else around[n - far + s]
 
@@ -202,10 +216,14 @@
                 sg[way, old, s, h] = own.astype(BF16)
             g_copy(u, s, way, s > 0).start()
 
-            @pl.when(lax.rem(e, far) == lax.rem(j, far))
+    def relay_d(u, s):
+        j, slot = lax.rem(u, nc), lax.rem(u, UNITS_HELD)
+        k = lax.rem(j, far)
+        for way in range(2):
+            e = around[far - s] if way == 0 else around[n - far + s]
+
+            @pl.when(lax.rem(e, far) == k)
             def _():
-                k = lax.rem(j, far)
-
                 @pl.when(u >= far)
                 def _():
                     d_copy(j, way, s > 0).wait_send()
@@ -226,18 +244,21 @@
         wide = g.astype(F32)
         ss[...] += jnp.sum((wide * wide).reshape(-1, *ss.shape), 0)
 
-    def arrive(u):
-        j, slot, old, layer = lax.rem(u, nc), lax.rem(u, UNITS_HELD), lax.rem(u, 4), 1 - u // nc
-        k = lax.rem(j, far)
+    def arrive_g(u):
+        j, slot, new, layer = lax.rem(u, nc), lax.rem(u, UNITS_HELD), lax.rem(u, RECEIVED), 1 - u // nc
         for way in range(2):
             g_copy(u, far - 1, way, True).wait_recv()
         for h, out in enumerate((og, ou)):
             own = pg[slot, pl.ds(pl.multiple_of(me * rows, rows), rows), h * FC:(h + 1) * FC]
-            own = (own + rg[0, old, far - 1, h].astype(F32) + rg[1, old, far - 1, h].astype(F32)).astype(BF16)
+            own = (own + rg[0, new, far - 1, h].astype(F32) + rg[1, new, far - 1, h].astype(F32)).astype(BF16)
             for s in range(2):
                 piece = own[:, s * LB:(s + 1) * LB]
                 out[layer, :, at_block(block(j) + s * nc)] = piece
                 square(piece)
+
+    def arrive_d(u):
+        j, slot, layer = lax.rem(u, nc), lax.rem(u, UNITS_HELD), 1 - u // nc
+        k = lax.rem(j, far)
 
         @pl.when(lax.rem(me, far) == k)
         def _():
@@ -252,17 +273,24 @@
                 for s in range(tall // LB):
                     square(own[:, s * LB:(s + 1) * LB])
 
-    def turn_round(at_step):
-        p, q = at_step // far, lax.rem(at_step, far)
-
-        @pl.when((q == 0) & (p >= 6) & (p < units + 6))
-        def _():
-            arrive(p - 6)
-
-        for when, s, lag in ((0, 0, 1), (1, 1, 2), (2, 2, 3), (3, 3, 4)):
-            @pl.when((q == when) & (p >= lag) & (p < units + lag))
-            def _(s=s, lag=lag):
-                relay(p - lag, s)
+    def go_on(kind, u, s):
+        if s == far:
+            (arrive_g if kind == "g" else arrive_d)(u)
+        else:
+            (relay_g if kind == "g" else relay_d)(u, s)
+
+    def turn_round(place, first, end):
+        for s in range(far, -1, -1):
+            here = [p for p in PLACES[s] if first <= p < end]
+            if not here:
+                continue
+            u = sum((place > p).astype(jnp.int32) for p in here) + PLACES[s].index(here[0])
+            due = functools.reduce(jnp.logical_or, [place == p for p in here])
+
+            @pl.when(due)
+            def _(s=s, u=u):
+                go_on("g", u, s)
+                go_on("d", u, s)
 
     def elementwise(gu, dh, slot):
         g, u = gu[:, :FC], gu[:, FC:]
@@ -304,6 +332,7 @@
             g[...] = jnp.zeros_like(g)
 
     per_chunk = nt // 2
+    steps = nc * per_chunk
     pl.semaphore_wait(barrier, n - 1)
 
     for t in range(2):
@@ -335,7 +364,7 @@
         turn(1, jn, t)
         front2(j, t + 1, 1)
         back_g(j, t, 0, t == 0)
-        turn_round(i)
+        turn_round(i, 0, steps)
 
     to_states(nc - 1, nt - 1, 1)
     back_d(nc - 1, nt - 1, 1)
@@ -361,6 +390,10 @@
         dyt[t] = dh1.T
         gu_in(t).start()
         a1t_in(t).wait()
+
+        @pl.when(lax.rem(t, 2) == 1)
+        def _():
+            turn_round(steps + t // 2, steps, steps + far)
 
     for t in range(2):
         turn(0, 0, t)
@@ -390,7 +423,7 @@
             for s in range(2):
                 gu_in(2 * i + s + nt).start()
 
-        turn_round(nc * per_chunk + i)
+        turn_round(steps + far + i, steps + far, 2 * steps + far)
 
     back_d(2 * nc - 1, nt - 1, 1)
     back_g(2 * nc - 1, nt - 1, 1)
@@ -415,9 +448,8 @@
         for copy in moment_copies(k):
             copy.start()
 
-    @pl.loop(units * far, (units + 5) * far + 1)
-    def _(at_step):
-        turn_round(at_step)
+    for kind, u, s in LAST:
+        go_on(kind, jnp.int32(u), s)
 
     tots[pl.ds(me, 1)] = ss[...][None]
     totals = [
@@ -529,10 +561,10 @@
         v_((nt, TT, d), BF16), v_((nt, d, TT), BF16), v_((nt, TT, d), BF16), v_((nt, TT, d), BF16), v_((nt, d, TT), BF16),
         v_((2 * nc, TT, LB), BF16), v_((TT, FC), BF16), v_((TT, FC), BF16), v_((TT, 2 * FC), BF16), v_((TT, 2 * FC), BF16),
         v_((UNITS_HELD, d, 2 * FC), F32), v_((UNITS_HELD, 2, d, LB), F32),
-        v_((2, 4, far, 2, rows, FC), BF16), v_((2, 2, far, 2, rows, FC), BF16),
+        v_((2, RECEIVED, far, 2, rows, FC), BF16), v_((2, 2, far, 2, rows, FC), BF16),
         v_((layers, rows, f), BF16), v_((layers, rows, f), BF16), v_((layers, f // n, d), BF16), v_((8, LB), F32), v_((n, 8, LB), F32),
         dma((layers, 3)), dma((nt,)), dma((nt,)), dma((2,)), dma((2 * nc + 6,)), dma((nt,)),
-        dma((2, 4, far)), dma((2, far)), dma((2, 2, far)), dma((2, far)), dma((n,)), dma((n,)),
+        dma((2, RECEIVED, far)), dma((2, far)), dma((2, 2, far)), dma((2, far)), dma((n,)), dma((n,)),
         dma((pieces, n)), dma((2, far, pieces)), dma((2, far, pieces)),
     ]
     kept_bytes = 2 * sum(one.size for one in w) + 4 * tokens * d

time: 356 us -> 352 us (0.989)
  Pallas kernels: 355 us -> 351 us
    pallas_call x1, Pallas kernels: 348 us -> 345 us  [train_step(): pl.pallas_call(functools.partial(step_kernel, nt, nc, n, sum((one.size fo...]
where the time goes in v8:
time: 352 us
  Pallas kernels  351 us (100%)
    pallas_call x1, Pallas kernels, train_step(): pl.pallas_call(functools.partial(step_kernel, nt, nc, n, sum((one.size fo...  345 us

profile of v8, /device:TPU:22, one launch (start us, length us, event | category | flops | bytes accessed | tf_op | source)
XLA Modules:
  0.0 352.3 jit_solution(8010094689158791706)
XLA Ops:
  0.6 344.6 %train_step.1 = (bf16[2,512,2048]{2,1,0:T(8,128)(2,1)S(1)}, bf16[2,512,2048]{2,1,0:T(8,128)(2,1)S(1)}, bf16[2,2048,512]{2,1,0:T(8,128)(2,1)S(1)}, f32[8,512,512]...) custom-call(bf16[1,4096,512]{2,1,0:T(8,128)(2,1)} %x_h.1, bf16[1,4096,512]{2,1,0:T(8,128)(2,1)} %dy_h.1, ...), custom_call_target="tpu_custom_call" | custom-call | tf_op jit(solution)/shard_map/train_step/pallas_call | solution.py:571
  345.3 6.8 %flush.1 = (bf16[2,512,2048]{2,1,0:T(8,128)(2,1)}, bf16[2,512,2048]{2,1,0:T(8,128)(2,1)}, bf16[2,2048,512]{2,1,0:T(8,128)(2,1)}, f32[2,64,2048]{2,1,0:T(8,128)},...) custom-call(bf16[2,512,2048]{2,1,0:T(8,128)(2,1)S(1)} %get-tuple-ele, ...), custom_call_target="tpu_custom_call" | custom-call | tf_op jit(solution)/shard_map/flush/pallas_call | solution.py:582

commit v9 on v8

--- a/solution.py
+++ b/solution.py
@@ -11,23 +11,29 @@
 MESH = pl.DeviceIdType.MESH
 TT = 512
 LB = 128
+EARLY = 2
+STAGED = 4
 FC = 2 * LB
 RECEIVED = 6
 UNITS_HELD = 7
 VMEM_BYTES = 67_043_328
-PLACES = (
-    (4, 8, 13, 16, 20, 25, 28, 33, 40, 44, 48, 52, 56, 61, 64),
-    (6, 11, 16, 19, 23, 28, 35, 39, 46, 48, 54, 57, 60, 66),
-    (9, 14, 18, 24, 26, 31, 41, 45, 51, 53, 59, 63, 64),
-    (12, 17, 21, 29, 30, 36, 48, 50, 56, 61, 65),
-    (18, 20, 31, 37, 41, 49, 53, 56, 63),
-)
-LAST = (
-    ("g", 9, 4), ("g", 15, 0), ("g", 11, 3), ("g", 12, 3), ("d", 15, 0), ("d", 9, 4), ("d", 11, 3), ("d", 12, 3), ("d", 14, 1),
-    ("d", 13, 2), ("g", 14, 1), ("g", 10, 4), ("d", 10, 4), ("g", 15, 1), ("g", 13, 2), ("g", 11, 4), ("g", 12, 4), ("d", 15, 1),
-    ("d", 14, 2), ("g", 14, 2), ("d", 11, 4), ("g", 15, 2), ("d", 13, 3), ("d", 12, 4), ("g", 13, 3), ("d", 15, 2), ("d", 14, 3),
-    ("g", 14, 3), ("g", 15, 3), ("d", 15, 3), ("d", 13, 4), ("g", 13, 4), ("d", 14, 4), ("g", 14, 4), ("g", 15, 4), ("d", 15, 4),
-)
+PLACES = tuple(tuple(int(p) for p in line.split(",")) for line in (
+    "4,8,12,17,20,24,29,33,40,44,48,52,56,60,64",
+    "6,11,15,21,23,27,34,39,46,47,53,57,61,65",
+    "9,14,19,25,26,30,42,45,50,56,58,62,66",
+    "12,17,22,30,34,37,49,51,55,60,63",
+    "15,20,30,43,46,47,54,57,62",
+))
+LAST = tuple((what[0], *(int(p) for p in what[1:].split("."))) for line in (
+    "d9.4,d11.3,g15.0,d15.0,d14.1,g9.4,g14.1,g11.3,d13.2,g12.3",
+    "d12.3,g15.1,d15.1,d10.4,g13.2,g14.2,d11.4,d14.2,g10.4,g11.4",
+    "g15.2,d15.2,g13.3,d13.3,d14.3,g14.3,d12.4,g15.3,d15.3,d13.4",
+    "g12.4,g13.4,g14.4,d14.4,g15.4,d15.4",
+) for what in line.split(","))
+EARLY_PLACES = tuple((what[0], *(int(p) for p in what[1:].split("."))) for line in (
+    "m1.2.1,m0.3.4,m1.3.6,s0.0.15,s0.1.19,s1.0.20,s0.2.23,s1.1.24",
+    "s1.2.28,s0.3.29,s1.3.31",
+) for what in line.split(","))
 
 
 def dot(a, b):
@@ -43,10 +49,11 @@
 
 
 def step_kernel(nt, nc, n, count, x_h, dy_h, wg_h, wu_h, wd_h, mg_h, mu_h, md_h, vg_h, vu_h, vd_h,
-                fg, fu, fd, wide_ref, gu_h, a1t_h,
+                fg, fu, fd, wide_ref, gu_h, a1t_h, mv_h, gs_h,
                 wgut, wdt, a, at, h1, dy, dyt, hid, hd0, hd1, dgu0, dgu1,
-                pg, pd, rg, sg, og, ou, od, ss, tots,
-                sem_w, sem_x, sem_dy, sem_at, sem_gu, sem_gi, rg_sem, rd_sem, sg_sem, sd_sem, ts_sem, tr_sem, mv_sem, ag_send, ag_recv):
+                pg, pd, rg, sg, gs, og, ou, od, ss, tots,
+                sem_w, sem_x, sem_dy, sem_at, sem_gu, sem_gi, rg_sem, rd_sem, sg_sem, sd_sem, ts_sem, tr_sem, mv_sem, ag_send, ag_recv,
+                free_sem, early_sem, ms_sem, mr_sem, gs_sem, gr_sem, late_sem):
     half, far = nc // 2, n // 2
     units = 2 * nc
     rows = pg.shape[1] // n
@@ -57,6 +64,10 @@
     around = [lax.rem(me + k, n) for k in range(n)]
     towards = (around[1], around[n - 1])
 
+    barrier = pltpu.get_barrier_semaphore()
+    for k in range(1, n):
+        pl.semaphore_signal(barrier, inc=1, device_id={"dp": around[k]}, device_id_type=MESH)
+
     def block(j):
         return 2 * lax.rem(j, half) + j // half
 
@@ -94,6 +105,40 @@
     def a1t_out(t):
         p = lax.rem(t, 2)
         return pltpu.make_async_copy(wgut.at[p], a1t_h.at[t], sem_at.at[p])
+
+    def hand_on(own, copies_h, send, recv, j, s, way, coming=False):
+        back_by = s + coming
+        origin = around[(n - back_by) % n] if way == 0 else around[back_by]
+        there = copies_h.at[j, origin]
+        here = there if back_by else own
+        if s == far - 1:
+            size = there.shape[0] // 2
+            there, here = there.at[pl.ds(way * size, size)], here.at[pl.ds(way * size, size)]
+        return pltpu.make_async_remote_copy(
+            here, there, send.at[way, s, j], recv.at[way, s, j], device_id={"dp": towards[way]}, device_id_type=MESH)
+
+    def moments_on(j, s, way, coming=False):
+        return hand_on(pd.at[STAGED, j], mv_h, ms_sem, mr_sem, j, s, way, coming)
+
+    def sums_on(j, s, way, coming=False):
+        return hand_on(gs.at[j], gs_h, gs_sem, gr_sem, j, s, way, coming)
+
+    def forward_on(which, j, s):
+        for way in range(2):
+            if s > 0:
+                which(j, s - 1, way, True).wait_recv()
+            which(j, s, way).start()
+
+    def early_moments():
+        copies = []
+        for j in range(EARLY):
+            for i, pair in enumerate(((mg_h, vg_h), (mu_h, vu_h))):
+                for c, h in enumerate(pair):
+                    for b in range(2):
+                        part = 4 * i + 2 * c + b
+                        copies.append(pltpu.make_async_copy(
+                            h.at[1, :, at_block(static_block(j) + b * nc)], pd.at[STAGED, j, pl.ds(part * rows, rows), :], early_sem.at[j, part]))
+        return copies
 
     def static_block(j):
         return 2 * (j % half) + j // half
@@ -152,16 +197,29 @@
     for t in range(1, nt):
         x_copy(t).start()
         dy_copy(t).start()
+    for copy in early_moments():
+        copy.start()
     for copy in w_copies(1):
         copy.start()
     forward(0, 0, False)
+    for copy in early_moments():
+        copy.wait()
+    pl.semaphore_wait(barrier, n - 1)
+    for j in range(EARLY):
+        forward_on(moments_on, j, 0)
 
     @pl.loop(0, nt // 2 - 1)
     def _(i):
         forward(2 * i + 1, 1, True)
         forward(2 * i + 2, 0, True)
 
+        for j in range(EARLY):
+            @pl.when(i == j + 1)
+            def _(j=j):
+                forward_on(moments_on, j, 1)
+
     forward(nt - 1, 1, True)
+    forward_on(moments_on, 0, 2)
     dy_copy(nt - 1).wait()
     finish(nt - 1, down())
     for copy in gu_out_all(nt - 2, 0):
@@ -173,9 +231,8 @@
     for copy in w_copies(1):
         copy.wait()
 
-    barrier = pltpu.get_barrier_semaphore()
-    for k in range(1, n):
-        pl.semaphore_signal(barrier, inc=1, device_id={"dp": around[k]}, device_id_type=MESH)
+    for other in towards:
+        pl.semaphore_signal(free_sem, inc=1, device_id={"dp": other}, device_id_type=MESH)
 
     def g_copy(u, s, way, both):
         part = (lambda ref: ref) if both else (lambda ref: ref.at[way])
@@ -255,6 +312,10 @@
                 piece = own[:, s * LB:(s + 1) * LB]
                 out[layer, :, at_block(block(j) + s * nc)] = piece
                 square(piece)
+
+            @pl.when(u < EARLY)
+            def _(own=own, h=h):
+                gs[jnp.minimum(u, EARLY - 1), h] = own
 
     def arrive_d(u):
         j, slot, layer = lax.rem(u, nc), lax.rem(u, UNITS_HELD), 1 - u // nc
@@ -333,7 +394,7 @@
 
     per_chunk = nt // 2
     steps = nc * per_chunk
-    pl.semaphore_wait(barrier, n - 1)
+    pl.semaphore_wait(free_sem, 2)
 
     for t in range(2):
         turn(1, 0, t)
@@ -365,6 +426,21 @@
         front2(j, t + 1, 1)
         back_g(j, t, 0, t == 0)
         turn_round(i, 0, steps)
+        @pl.when(i == STAGED * per_chunk - 1)
+        def _():
+            for j in range(EARLY):
+                for way in range(2):
+                    moments_on(j, 0, way).wait_send()
+
+        for kind, which in (("m", moments_on), ("s", sums_on)):
+            due = [what for what in EARLY_PLACES if what[0] == kind]
+
+            @pl.when((i >= due[0][3]) & (i <= due[-1][3]))
+            def _(which=which, due=due):
+                for _, j, s, place in due:
+                    @pl.when(i == place)
+                    def _(j=j, s=s):
+                        forward_on(which, j, s)
 
     to_states(nc - 1, nt - 1, 1)
     back_d(nc - 1, nt - 1, 1)
@@ -450,6 +526,23 @@
 
     for kind, u, s in LAST:
         go_on(kind, jnp.int32(u), s)
+
+    def early_loads(k):
+        made = []
+        for j in range(EARLY):
+            made.append(pltpu.make_async_copy(mv_h.at[j, around[k]], pd.at[k - 1, j], late_sem.at[k - 1, j, 0]))
+            made.append(pltpu.make_async_copy(gs_h.at[j, around[k]], rg.at[j, (k - 1) // far, (k - 1) % far], late_sem.at[k - 1, j, 1]))
+        return made
+
+    for which in (moments_on, sums_on):
+        for j in range(EARLY):
+            for way in range(2):
+                which(j, far - 1, way, True).wait_recv()
+                for s in range(which is moments_on, far):
+                    which(j, s, way).wait_send()
+    for k in range(1, n):
+        for copy in early_loads(k):
+            copy.start()
 
     tots[pl.ds(me, 1)] = ss[...][None]
     totals = [
@@ -479,13 +572,18 @@
             start += part * tall
         return pl.ds(pl.multiple_of(start, tall), tall)
 
-    def pass_on(k, s, way, coming=False):
-        i, layer = pieces[k]
+    early = sorted(static_block(j) + s * nc for j in range(EARLY) for s in range(2))
+    between = [(p + 1, q) for p, q in zip([-1] + early, early + [2 * nc]) if q > p + 1]
+    parcels = [(k, i, layer, cols) for k, (i, layer) in enumerate(pieces)
+               for cols in ([pl.ds(p * LB, (q - p) * LB) for p, q in between] if layer == 1 and i < 2 else [slice(None)])]
+
+    def pass_on(c, s, way, coming=False):
+        _, i, layer, cols = parcels[c]
         back_by = s + coming
         origin = around[(n - back_by) % n] if way == 0 else around[back_by]
-        here = full[i].at[layer, rows_of(i, origin, way if s == far - 1 else None), :]
+        here = full[i].at[layer, rows_of(i, origin, way if s == far - 1 else None), cols]
         return pltpu.make_async_remote_copy(
-            here, here, ag_send.at[way, s, k], ag_recv.at[way, s, k], device_id={"dp": towards[way]}, device_id_type=MESH)
+            here, here, ag_send.at[way, s, c], ag_recv.at[way, s, c], device_id={"dp": towards[way]}, device_id_type=MESH)
 
     for k, (i, layer) in enumerate(pieces):
         def adamw(here, where_g, where_w):
@@ -506,21 +604,41 @@
             else:
                 cols = pl.ds(b * d, d)
                 adamw(here, (slice(None), cols), (pl.ds(pl.multiple_of(me * rows, rows), rows), cols))
-        for way in range(2):
-            pass_on(k, 0, way).start()
+        for c, parcel in enumerate(parcels):
+            if parcel[0] == k:
+                for way in range(2):
+                    pass_on(c, 0, way).start()
+
+    for k in range(1, n):
+        for copy in early_loads(k):
+            copy.wait()
+
+    @pl.loop(1, n)
+    def _(k):
+        origin = lax.rem(me + k, n)
+        mine = pl.ds(pl.multiple_of(origin * rows, rows), rows)
+        for j in range(EARLY):
+            for i, f in enumerate((fg, fu)):
+                for b in range(2):
+                    cols = at_block(static_block(j) + b * nc)
+                    g = rg[j, (k - 1) // far, lax.rem(k - 1, far), i, :, b * LB:(b + 1) * LB].astype(F32) * factor
+                    m = 0.9 * pd[k - 1, j, (4 * i + b) * rows:(4 * i + b + 1) * rows, :] + 0.1 * g
+                    v = 0.95 * pd[k - 1, j, (4 * i + 2 + b) * rows:(4 * i + 3 + b) * rows, :] + 0.05 * g * g
+                    w = f[1, mine, cols].astype(F32)
+                    f[1, mine, cols] = (w - 0.02 * (m * lax.rsqrt(v + 1e-8) + 0.1 * w)).astype(BF16)
 
     for s in range(far):
-        for k in range(len(pieces)):
+        for c in range(len(parcels)):
             for way in range(2):
-                pass_on(k, s, way, True).wait_recv()
+                pass_on(c, s, way, True).wait_recv()
                 if s + 1 < far:
-                    pass_on(k, s + 1, way).start()
+                    pass_on(c, s + 1, way).start()
     for copy in totals:
         copy.wait_send()
     for s in range(far):
-        for k in range(len(pieces)):
+        for c in range(len(parcels)):
             for way in range(2):
-                pass_on(k, s, way).wait_send()
+                pass_on(c, s, way).wait_send()
 
 
 def flush_kernel(n, fg, fu, fd, wide, *refs):
@@ -551,6 +669,7 @@
     nt, nc = tokens // TT, f // FC
     far, rows = n // 2, d // n
     pieces = 3 * layers
+    parcels = pieces + 2 * 2 * EARLY
     hbm = pl.BlockSpec(memory_space=pl.ANY)
     vmem = pl.BlockSpec(memory_space=pltpu.VMEM)
     shape = jax.ShapeDtypeStruct
@@ -561,19 +680,22 @@
         v_((nt, TT, d), BF16), v_((nt, d, TT), BF16), v_((nt, TT, d), BF16), v_((nt, TT, d), BF16), v_((nt, d, TT), BF16),
         v_((2 * nc, TT, LB), BF16), v_((TT, FC), BF16), v_((TT, FC), BF16), v_((TT, 2 * FC), BF16), v_((TT, 2 * FC), BF16),
         v_((UNITS_HELD, d, 2 * FC), F32), v_((UNITS_HELD, 2, d, LB), F32),
-        v_((2, RECEIVED, far, 2, rows, FC), BF16), v_((2, 2, far, 2, rows, FC), BF16),
+        v_((2, RECEIVED, far, 2, rows, FC), BF16), v_((2, 2, far, 2, rows, FC), BF16), v_((EARLY, 2, rows, FC), BF16),
         v_((layers, rows, f), BF16), v_((layers, rows, f), BF16), v_((layers, f // n, d), BF16), v_((8, LB), F32), v_((n, 8, LB), F32),
         dma((layers, 3)), dma((nt,)), dma((nt,)), dma((2,)), dma((2 * nc + 6,)), dma((nt,)),
         dma((2, RECEIVED, far)), dma((2, far)), dma((2, 2, far)), dma((2, far)), dma((n,)), dma((n,)),
-        dma((pieces, n)), dma((2, far, pieces)), dma((2, far, pieces)),
+        dma((pieces, n)), dma((2, far, parcels)), dma((2, far, parcels)),
+        pltpu.SemaphoreType.REGULAR, dma((EARLY, 8)), dma((2, far, EARLY)), dma((2, far, EARLY)), dma((2, far, EARLY)), dma((2, far, EARLY)),
+        dma((n - 1, EARLY, 2)),
     ]
     kept_bytes = 2 * sum(one.size for one in w) + 4 * tokens * d
-    *new, wide, _, _ = pl.pallas_call(
+    *new, wide, _, _, _, _ = pl.pallas_call(
         functools.partial(step_kernel, nt, nc, n, sum(one.size for one in w)),
         name="train_step",
-        out_shape=kept + [shape((nc, nt, TT, 2 * FC), F32), shape((nt, d, TT), BF16)],
+        out_shape=kept + [shape((nc, nt, TT, 2 * FC), F32), shape((nt, d, TT), BF16),
+                          shape((EARLY, n, d, LB), F32), shape((EARLY, n, 2, rows, FC), BF16)],
         in_specs=[hbm] * 11,
-        out_specs=[vmem] * 4 + [hbm] * 2,
+        out_specs=[vmem] * 4 + [hbm] * 4,
         scratch_shapes=scratch,
         compiler_params=pltpu.CompilerParams(vmem_limit_bytes=VMEM_BYTES - kept_bytes, collective_id=0, has_side_effects=True),
     )(x, dy, *w, *m, *v)

time: 352 us -> 350 us (level)
  no operation moved by 1% of the time
where the time goes in v9:
time: 350 us
  Pallas kernels  349 us (100%)
    pallas_call x1, Pallas kernels, train_step(): pl.pallas_call(functools.partial(step_kernel, nt, nc, n, sum((one.size fo...  342 us

profile of v9, /device:TPU:22, one launch (start us, length us, event | category | flops | bytes accessed | tf_op | source)
XLA Modules:
  0.0 349.6 jit_solution(779453655507161758)
XLA Ops:
  0.6 341.9 %train_step.1 = (bf16[2,512,2048]{2,1,0:T(8,128)(2,1)S(1)}, bf16[2,512,2048]{2,1,0:T(8,128)(2,1)S(1)}, bf16[2,2048,512]{2,1,0:T(8,128)(2,1)S(1)}, f32[8,512,512]...) custom-call(bf16[1,4096,512]{2,1,0:T(8,128)(2,1)} %x_h.1, ...), custom_call_target="tpu_custom_call" | custom-call | tf_op jit(solution)/shard_map/train_step/pallas_call | solution.py:692
  342.6 6.8 %flush.1 = (bf16[2,512,2048]{2,1,0:T(8,128)(2,1)}, bf16[2,512,2048]{2,1,0:T(8,128)(2,1)}, bf16[2,2048,512]{2,1,0:T(8,128)(2,1)}, f32[2,64,2048]{2,1,0:T(8,128)},...) custom-call(bf16[2,512,2048]{2,1,0:T(8,128)(2,1)S(1)} %get-tuple-ele, ...), custom_call_target="tpu_custom_call" | custom-call | tf_op jit(solution)/shard_map/flush/pallas_call | solution.py:704

commit v10 on v9

--- a/solution.py
+++ b/solution.py
@@ -18,20 +18,20 @@
 UNITS_HELD = 7
 VMEM_BYTES = 67_043_328
 PLACES = tuple(tuple(int(p) for p in line.split(",")) for line in (
-    "4,8,12,17,20,24,29,33,40,44,48,52,56,60,64",
-    "6,11,15,21,23,27,34,39,46,47,53,57,61,65",
-    "9,14,19,25,26,30,42,45,50,56,58,62,66",
-    "12,17,22,30,34,37,49,51,55,60,63",
-    "15,20,30,43,46,47,54,57,62",
+    "4,8,12,16,20,24,29,33,40,44,48,52,56,60,64",
+    "6,11,15,21,23,27,36,41,45,47,53,57,61,66",
+    "9,14,18,25,29,30,42,45,50,54,59,63,65",
+    "12,17,21,31,35,37,49,51,56,62,63",
+    "15,20,27,41,46,48,54,57,61",
 ))
 LAST = tuple((what[0], *(int(p) for p in what[1:].split("."))) for line in (
-    "d9.4,d11.3,g15.0,d15.0,d14.1,g9.4,g14.1,g11.3,d13.2,g12.3",
-    "d12.3,g15.1,d15.1,d10.4,g13.2,g14.2,d11.4,d14.2,g10.4,g11.4",
-    "g15.2,d15.2,g13.3,d13.3,d14.3,g14.3,d12.4,g15.3,d15.3,d13.4",
-    "g12.4,g13.4,g14.4,d14.4,g15.4,d15.4",
+    "g15.0,g11.3,d14.1,d15.0,d9.4,d11.3,d12.3,d13.2,g14.1,g12.3",
+    "d10.4,g15.1,d15.1,g13.2,g9.4,d14.2,g14.2,g10.4,d11.4,d12.4",
+    "g11.4,g15.2,d15.2,g12.4,d13.3,g13.3,g14.3,d14.3,g15.3,d15.3",
+    "g13.4,d13.4,d14.4,g14.4,g15.4,d15.4",
 ) for what in line.split(","))
 EARLY_PLACES = tuple((what[0], *(int(p) for p in what[1:].split("."))) for line in (
-    "m1.2.1,m0.3.4,m1.3.6,s0.0.15,s0.1.19,s1.0.20,s0.2.23,s1.1.24",
+    "m1.2.0,m0.3.4,m1.3.6,s0.0.15,s0.1.19,s1.0.20,s1.1.23,s0.2.24",
     "s1.2.28,s0.3.29,s1.3.31",
 ) for what in line.split(","))
 
@@ -106,28 +106,56 @@
         p = lax.rem(t, 2)
         return pltpu.make_async_copy(wgut.at[p], a1t_h.at[t], sem_at.at[p])
 
-    def hand_on(own, copies_h, send, recv, j, s, way, coming=False):
+    def origin_of(s, way):
+        return around[(n - s) % n] if way == 0 else around[s]
+
+    def half_of(ref, s, way):
+        size = ref.shape[0] // 2
+        return ref.at[pl.ds(way * size, size)] if s == far - 1 else ref
+
+    def kept_moments(j, s, way):
+        return pd.at[2 * s + j, way] if s < 2 else mv_h.at[j, origin_of(s + 1, way)]
+
+    def moments_on(j, s, way):
+        here = kept_moments(j, s - 1, way) if s else pd.at[STAGED, j]
+        there = pd.at[2 * s + j, way] if s < 2 else mv_h.at[j, origin_of(s, way)]
+        return pltpu.make_async_remote_copy(
+            half_of(here, s, way), half_of(there, s, way), ms_sem.at[way, s, j], mr_sem.at[way, s, j],
+            device_id={"dp": towards[way]}, device_id_type=MESH)
+
+    def moments_in(j, s, way):
+        here = half_of(kept_moments(j, s, way), s, way)
+        return pltpu.make_async_remote_copy(
+            here, here, ms_sem.at[way, s, j], mr_sem.at[way, s, j], device_id={"dp": towards[way]}, device_id_type=MESH)
+
+    def moments_out(j, s, way):
+        return pltpu.make_async_copy(kept_moments(j, s, way), mv_h.at[j, origin_of(s + 1, way)], early_sem.at[j, 2 * s + way])
+
+    def moments_left(j, s):
+        for way in range(2):
+            moments_on(j, s, way).wait_send()
+            if s:
+                moments_out(j, s - 1, way).wait()
+
+    def sums_on(j, s, way, coming=False):
         back_by = s + coming
-        origin = around[(n - back_by) % n] if way == 0 else around[back_by]
-        there = copies_h.at[j, origin]
-        here = there if back_by else own
-        if s == far - 1:
-            size = there.shape[0] // 2
-            there, here = there.at[pl.ds(way * size, size)], here.at[pl.ds(way * size, size)]
+        there = gs_h.at[j, origin_of(back_by, way)]
+        here = there if back_by else gs.at[j]
         return pltpu.make_async_remote_copy(
-            here, there, send.at[way, s, j], recv.at[way, s, j], device_id={"dp": towards[way]}, device_id_type=MESH)
-
-    def moments_on(j, s, way, coming=False):
-        return hand_on(pd.at[STAGED, j], mv_h, ms_sem, mr_sem, j, s, way, coming)
-
-    def sums_on(j, s, way, coming=False):
-        return hand_on(gs.at[j], gs_h, gs_sem, gr_sem, j, s, way, coming)
+            half_of(here, s, way), half_of(there, s, way), gs_sem.at[way, s, j], gr_sem.at[way, s, j],
+            device_id={"dp": towards[way]}, device_id_type=MESH)
+
+    def sums_in(j, s, way):
+        return sums_on(j, s, way, True)
 
     def forward_on(which, j, s):
         for way in range(2):
+            moments = which is moments_on
             if s > 0:
-                which(j, s - 1, way, True).wait_recv()
+                (moments_in if moments else sums_in)(j, s - 1, way).wait_recv()
             which(j, s, way).start()
+            if moments and 0 < s < 3:
+                moments_out(j, s - 1, way).start()
 
     def early_moments():
         copies = []
@@ -211,12 +239,16 @@
     @pl.loop(0, nt // 2 - 1)
     def _(i):
         forward(2 * i + 1, 1, True)
+
+        @pl.when(i == 2)
+        def _():
+            forward_on(moments_on, 1, 1)
+
         forward(2 * i + 2, 0, True)
 
-        for j in range(EARLY):
-            @pl.when(i == j + 1)
-            def _(j=j):
-                forward_on(moments_on, j, 1)
+        @pl.when(i == 1)
+        def _():
+            forward_on(moments_on, 0, 1)
 
     forward(nt - 1, 1, True)
     forward_on(moments_on, 0, 2)
@@ -395,6 +427,7 @@
     per_chunk = nt // 2
     steps = nc * per_chunk
     pl.semaphore_wait(free_sem, 2)
+    moments_left(0, 1)
 
     for t in range(2):
         turn(1, 0, t)
@@ -426,11 +459,11 @@
         front2(j, t + 1, 1)
         back_g(j, t, 0, t == 0)
         turn_round(i, 0, steps)
-        @pl.when(i == STAGED * per_chunk - 1)
-        def _():
-            for j in range(EARLY):
-                for way in range(2):
-                    moments_on(j, 0, way).wait_send()
+        for chunk, whose in ((1, ((1, 1),)), (2, ((0, 2),)), (3, ((1, 2),)), (STAGED, ((0, 0), (1, 0)))):
+            @pl.when(i == chunk * per_chunk - 1)
+            def _(whose=whose):
+                for j, s in whose:
+                    moments_left(j, s)
 
         for kind, which in (("m", moments_on), ("s", sums_on)):
             due = [what for what in EARLY_PLACES if what[0] == kind]
@@ -534,12 +567,13 @@
             made.append(pltpu.make_async_copy(gs_h.at[j, around[k]], rg.at[j, (k - 1) // far, (k - 1) % far], late_sem.at[k - 1, j, 1]))
         return made
 
-    for which in (moments_on, sums_on):
-        for j in range(EARLY):
-            for way in range(2):
-                which(j, far - 1, way, True).wait_recv()
-                for s in range(which is moments_on, far):
-                    which(j, s, way).wait_send()
+    for j in range(EARLY):
+        for way in range(2):
+            moments_in(j, far - 1, way).wait_recv()
+            moments_on(j, far - 1, way).wait_send()
+            sums_in(j, far - 1, way).wait_recv()
+            for s in range(far):
+                sums_on(j, s, way).wait_send()
     for k in range(1, n):
         for copy in early_loads(k):
             copy.start()

time: 350 us -> 350 us (level)
  no operation moved by 1% of the time
where the time goes in v10:
time: 350 us
  Pallas kernels  349 us (100%)
    pallas_call x1, Pallas kernels, train_step(): pl.pallas_call(functools.partial(step_kernel, nt, nc, n, sum((one.size fo...  342 us

profile of v10, /device:TPU:22, one launch (start us, length us, event | category | flops | bytes accessed | tf_op | source)
XLA Modules:
  0.0 349.8 jit_solution(15848064196452052811)
XLA Ops:
  0.6 342.1 %train_step.1 = (bf16[2,512,2048]{2,1,0:T(8,128)(2,1)S(1)}, bf16[2,512,2048]{2,1,0:T(8,128)(2,1)S(1)}, bf16[2,2048,512]{2,1,0:T(8,128)(2,1)S(1)}, f32[8,512,512]...) custom-call(bf16[1,4096,512]{2,1,0:T(8,128)(2,1)} %x_h.1, ...), custom_call_target="tpu_custom_call" | custom-call | tf_op jit(solution)/shard_map/train_step/pallas_call | solution.py:726
  342.8 6.8 %flush.1 = (bf16[2,512,2048]{2,1,0:T(8,128)(2,1)}, bf16[2,512,2048]{2,1,0:T(8,128)(2,1)}, bf16[2,2048,512]{2,1,0:T(8,128)(2,1)}, f32[2,64,2048]{2,1,0:T(8,128)},...) custom-call(bf16[2,512,2048]{2,1,0:T(8,128)(2,1)S(1)} %get-tuple-ele, ...), custom_call_target="tpu_custom_call" | custom-call | tf_op jit(solution)/shard_map/flush/pallas_call | solution.py:738

commit v11 on v10

--- a/solution.py
+++ b/solution.py
@@ -448,27 +448,29 @@
                 copy.wait()
 
         jk, tk, jn = k // nt, lax.rem(k, nt), jnp.minimum(j + 1, nc - 1)
+        back_g(jk, tk, 1)
         to_states(jk, tk, 1)
         back_d(jk, tk, 1)
         front2(j, t, 0)
         to_states(j, t, 0)
-        back_g(jk, tk, 1)
         turn(1, jn, t + 1)
         back_d(j, t, 0, t == 0)
+        front2(j, t + 1, 1)
         turn(1, jn, t)
-        front2(j, t + 1, 1)
         back_g(j, t, 0, t == 0)
         turn_round(i, 0, steps)
-        for chunk, whose in ((1, ((1, 1),)), (2, ((0, 2),)), (3, ((1, 2),)), (STAGED, ((0, 0), (1, 0)))):
-            @pl.when(i == chunk * per_chunk - 1)
-            def _(whose=whose):
-                for j, s in whose:
-                    moments_left(j, s)
+        @pl.when((lax.rem(i, per_chunk) == per_chunk - 1) & (i < STAGED * per_chunk))
+        def _():
+            for chunk, whose in ((1, ((1, 1),)), (2, ((0, 2),)), (3, ((1, 2),)), (STAGED, ((0, 0), (1, 0)))):
+                @pl.when(i == chunk * per_chunk - 1)
+                def _(whose=whose):
+                    for j, s in whose:
+                        moments_left(j, s)
 
         for kind, which in (("m", moments_on), ("s", sums_on)):
             due = [what for what in EARLY_PLACES if what[0] == kind]
 
-            @pl.when((i >= due[0][3]) & (i <= due[-1][3]))
+            @pl.when(functools.reduce(jnp.logical_or, [i == what[3] for what in due]))
             def _(which=which, due=due):
                 for _, j, s, place in due:
                     @pl.when(i == place)
@@ -567,6 +569,13 @@
             made.append(pltpu.make_async_copy(gs_h.at[j, around[k]], rg.at[j, (k - 1) // far, (k - 1) % far], late_sem.at[k - 1, j, 1]))
         return made
 
+    tots[pl.ds(me, 1)] = ss[...][None]
+    totals = [
+        pltpu.make_async_remote_copy(ss, tots.at[me], ts_sem.at[k], tr_sem.at[n - k], device_id={"dp": around[k]}, device_id_type=MESH)
+        for k in range(1, n)
+    ]
+    for copy in totals:
+        copy.start()
     for j in range(EARLY):
         for way in range(2):
             moments_in(j, far - 1, way).wait_recv()
@@ -577,14 +586,6 @@
     for k in range(1, n):
         for copy in early_loads(k):
             copy.start()
-
-    tots[pl.ds(me, 1)] = ss[...][None]
-    totals = [
-        pltpu.make_async_remote_copy(ss, tots.at[me], ts_sem.at[k], tr_sem.at[n - k], device_id={"dp": around[k]}, device_id_type=MESH)
-        for k in range(1, n)
-    ]
-    for copy in totals:
-        copy.start()
     for way in range(2):
         for s in range(far):
             for u in (units - 2, units - 1):

time: 350 us -> 349 us (level)
  no operation moved by 1% of the time
where the time goes in v11:
time: 349 us
  Pallas kernels  348 us (100%)
    pallas_call x1, Pallas kernels, train_step(): pl.pallas_call(functools.partial(step_kernel, nt, nc, n, sum((one.size fo...  342 us

profile of v11, /device:TPU:22, one launch (start us, length us, event | category | flops | bytes accessed | tf_op | source)
XLA Modules:
  0.0 349.3 jit_solution(1532300730655056359)
XLA Ops:
  0.6 341.6 %train_step.1 = (bf16[2,512,2048]{2,1,0:T(8,128)(2,1)S(1)}, bf16[2,512,2048]{2,1,0:T(8,128)(2,1)S(1)}, bf16[2,2048,512]{2,1,0:T(8,128)(2,1)S(1)}, f32[8,512,512]...) custom-call(bf16[1,4096,512]{2,1,0:T(8,128)(2,1)} %x_h.1, ...), custom_call_target="tpu_custom_call" | custom-call | tf_op jit(solution)/shard_map/train_step/pallas_call | solution.py:727
  342.2 6.8 %flush.1 = (bf16[2,512,2048]{2,1,0:T(8,128)(2,1)}, bf16[2,512,2048]{2,1,0:T(8,128)(2,1)}, bf16[2,2048,512]{2,1,0:T(8,128)(2,1)}, f32[2,64,2048]{2,1,0:T(8,128)},...) custom-call(bf16[2,512,2048]{2,1,0:T(8,128)(2,1)S(1)} %get-tuple-ele, ...), custom_call_target="tpu_custom_call" | custom-call | tf_op jit(solution)/shard_map/flush/pallas_call | solution.py:739

commit v12 on v11

--- a/solution.py
+++ b/solution.py
@@ -18,21 +18,21 @@
 UNITS_HELD = 7
 VMEM_BYTES = 67_043_328
 PLACES = tuple(tuple(int(p) for p in line.split(",")) for line in (
-    "4,8,12,16,20,24,29,33,40,44,48,52,56,60,64",
-    "6,11,15,21,23,27,36,41,45,47,53,57,61,66",
-    "9,14,18,25,29,30,42,45,50,54,59,63,65",
-    "12,17,21,31,35,37,49,51,56,62,63",
-    "15,20,27,41,46,48,54,57,61",
+    "4,8,13,16,20,24,29,32,40,44,48,52,56,60,64",
+    "6,11,15,22,23,27,36,41,46,47,53,57,61,66",
+    "9,14,18,26,29,30,42,45,50,55,59,62,65",
+    "12,17,21,31,33,37,49,51,55,61,63",
+    "15,20,25,42,45,46,55,57,62",
 ))
 LAST = tuple((what[0], *(int(p) for p in what[1:].split("."))) for line in (
-    "g15.0,g11.3,d14.1,d15.0,d9.4,d11.3,d12.3,d13.2,g14.1,g12.3",
-    "d10.4,g15.1,d15.1,g13.2,g9.4,d14.2,g14.2,g10.4,d11.4,d12.4",
-    "g11.4,g15.2,d15.2,g12.4,d13.3,g13.3,g14.3,d14.3,g15.3,d15.3",
+    "g15.0,g11.3,d14.1,g9.4,d15.0,d9.4,g10.4,g12.3,d11.3,d12.3",
+    "d10.4,g14.1,g15.1,d13.2,d15.1,d11.4,g13.2,g11.4,d14.2,g14.2",
+    "g12.4,g15.2,d13.3,d12.4,d15.2,d14.3,g13.3,g14.3,g15.3,d15.3",
     "g13.4,d13.4,d14.4,g14.4,g15.4,d15.4",
 ) for what in line.split(","))
 EARLY_PLACES = tuple((what[0], *(int(p) for p in what[1:].split("."))) for line in (
-    "m1.2.0,m0.3.4,m1.3.6,s0.0.15,s0.1.19,s1.0.20,s1.1.23,s0.2.24",
-    "s1.2.28,s0.3.29,s1.3.31",
+    "m1.2.1,m0.3.4,m1.3.7,s0.0.15,s0.1.19,s1.0.20,s1.1.23,s0.2.24",
+    "s1.2.27,s0.3.29,s1.3.31",
 ) for what in line.split(","))
 
 
@@ -681,7 +681,7 @@
     layers, d = fg.shape[0], fg.shape[1]
     rows, far = d // n, n // 2
     deep = far * rows
-    copies = []
+    copies = [(f.at[layer], out.at[layer]) for layer in range(layers) for f, out in zip((fg, fu, fd), outs)]
     for k, (i, layer) in enumerate((i, layer) for layer in (1, 0) for i in range(3)):
         for c in range(2):
             out = outs[3 + 3 * c + i]
@@ -689,7 +689,6 @@
                 copies.append((wide.at[k, pl.ds(c * deep, deep), :], out.at[layer]))
             else:
                 copies += [(wide.at[k, pl.ds(c * deep + b * rows, rows), :], out.at[layer, :, pl.ds(b * d, d)]) for b in range(far)]
-    copies += [(f.at[layer], out.at[layer]) for layer in range(layers) for f, out in zip((fg, fu, fd), outs)]
     copies = [pltpu.make_async_copy(*pair, sem.at[i]) for i, pair in enumerate(copies)]
     for copy in copies:
         copy.start()

time: 349 us -> 350 us (level)
  no operation moved by 1% of the time
where the time goes in v12:
time: 350 us
  Pallas kernels  349 us (100%)
    pallas_call x1, Pallas kernels, train_step(): pl.pallas_call(functools.partial(step_kernel, nt, nc, n, sum((one.size fo...  342 us

profile of v12, /device:TPU:22, one launch (start us, length us, event | category | flops | bytes accessed | tf_op | source)
XLA Modules:
  0.0 349.8 jit_solution(3092634273730905320)
XLA Ops:
  0.6 342.2 %train_step.1 = (bf16[2,512,2048]{2,1,0:T(8,128)(2,1)S(1)}, bf16[2,512,2048]{2,1,0:T(8,128)(2,1)S(1)}, bf16[2,2048,512]{2,1,0:T(8,128)(2,1)S(1)}, f32[8,512,512]...) custom-call(bf16[1,4096,512]{2,1,0:T(8,128)(2,1)} %x_h.1, ...), custom_call_target="tpu_custom_call" | custom-call | tf_op jit(solution)/shard_map/train_step/pallas_call | solution.py:726
  342.8 6.8 %flush.1 = (bf16[2,512,2048]{2,1,0:T(8,128)(2,1)}, bf16[2,512,2048]{2,1,0:T(8,128)(2,1)}, bf16[2,2048,512]{2,1,0:T(8,128)(2,1)}, f32[2,64,2048]{2,1,0:T(8,128)},...) custom-call(bf16[2,512,2048]{2,1,0:T(8,128)(2,1)S(1)} %get-tuple-ele, ...), custom_call_target="tpu_custom_call" | custom-call | tf_op jit(solution)/shard_map/flush/pallas_call | solution.py:738
